TPU v7x, 32 devices: a whole 2x2x4 slice. The times are simulated.
32 devices in a mesh: group: 2 (over y), cp: 8 (over z, x), hd: 2 (over core).
Axes of the slice: x: 2, y: 2, z: 4, core: 2. Of those that a mesh axis runs over, the one named last changes fastest.
Arguments:
- doc_lengths: int32 [8], P('group'), parts along dimension 0, may hold values from 1 to 384, 1024 in all
- queries: bfloat16 [2048, 4096], P(('group', 'cp'), 'hd'), parts along dimension 0, may hold values from -52 to 52
- key_states: bfloat16 [2048, 1024], P(('group', 'cp'), 'hd'), parts along dimension 0, may hold values from -4 to 4
- value_head_states: bfloat16 [2048, 1024], P(('group', 'cp'), 'hd'), parts along dimension 0, may hold values from -6 to 6
- out_grad: bfloat16 [2048, 4096], P(('group', 'cp'), 'hd'), parts along dimension 0, may hold values from -6 to 6
Outputs:
- attended: bfloat16 [2048, 4096], P(('group', 'cp'), 'hd'), parts along dimension 0
- grad_queries: bfloat16 [2048, 4096], P(('group', 'cp'), 'hd'), parts along dimension 0
- grad_keys: bfloat16 [2048, 1024], P(('group', 'cp'), 'hd'), parts along dimension 0
- grad_values: bfloat16 [2048, 1024], P(('group', 'cp'), 'hd'), parts along dimension 0
There are 2 independent parts, one for each index of `group`. A program takes and returns all parts, laid end to end along the dimension named above; each array names one. Nothing has to cross between parts.
Inputs may be any that keep to these rules, and one draw needn't show every extreme that they name: `doc_lengths`: documents lie end to end in token order; their lengths sum to 1024.
All inputs are finite; a program needn't handle non-finite values.
Results may differ from a plain program's by a relative error of at most 0.028.
Values may be sent and summed in bfloat16 or wider, within the bound.
No kernel may reach another device: no remote copies, remote signals or barrier semaphores. Data moves between devices by JAX's collectives and lax.ppermute only.
A program may use at most 64 MiB of HBM per device.

v0:
```python
import math

import jax
import jax.numpy as jnp
from jax import lax
from jax.sharding import PartitionSpec as P

HEAD_SIZE = 128
REACH = 3


masked_score = -1e30


def from_behind(value, axis, by):
    peers = lax.axis_size(axis)
    pairs = [(i, i + by) for i in range(peers) if 0 <= i + by < peers]
    return lax.ppermute(value, axis, pairs)


def document_ids(doc_lengths, positions):
    ends = jnp.cumsum(doc_lengths)
    counted = jnp.sum((ends[None, :] <= positions[:, None]).astype(jnp.int32), axis=1)
    return jnp.where(positions < 0, jnp.int32(-1), counted)


def attend(queries, window, out_grad, allowed):
    tok_rows = queries.shape[0]
    window_rows = window.shape[1]
    head_kv = window.shape[2] // HEAD_SIZE
    group_size = queries.shape[1] // window.shape[2]
    score_scale = 1.0 / math.sqrt(HEAD_SIZE)
    query_heads = queries.reshape(tok_rows, head_kv, group_size, HEAD_SIZE)
    key_heads = window[0].reshape(window_rows, head_kv, HEAD_SIZE)
    value_heads = window[1].reshape(window_rows, head_kv, HEAD_SIZE)
    grad_heads = out_grad.reshape(tok_rows, head_kv, group_size, HEAD_SIZE)
    scores = (
        jnp.einsum("qhgd,khd->hgqk", query_heads, key_heads, preferred_element_type=jnp.float32)
        * score_scale
    )
    scores = jnp.where(allowed, scores, masked_score)
    row_max = jnp.max(scores, axis=-1, keepdims=True)
    weights_raw = jnp.exp(scores - row_max)
    probs = weights_raw / jnp.sum(weights_raw, axis=-1, keepdims=True)
    probs_low = probs.astype(jnp.bfloat16)
    attended = jnp.einsum(
        "hgqk,khd->qhgd", probs_low, value_heads, preferred_element_type=jnp.float32
    ).astype(jnp.bfloat16)
    delta = jnp.sum(
        grad_heads.astype(jnp.float32) * attended.astype(jnp.float32), axis=-1
    ).transpose(1, 2, 0)
    grad_value = jnp.einsum(
        "hgqk,qhgd->khd", probs_low, grad_heads, preferred_element_type=jnp.float32
    )
    grad_probs = jnp.einsum(
        "qhgd,khd->hgqk", grad_heads, value_heads, preferred_element_type=jnp.float32
    )
    grad_scores = (probs * (grad_probs - delta[..., None])).astype(jnp.bfloat16)
    grad_query = (
        jnp.einsum("hgqk,khd->qhgd", grad_scores, key_heads, preferred_element_type=jnp.float32)
        * score_scale
    ).astype(jnp.bfloat16)
    grad_key = (
        jnp.einsum("hgqk,qhgd->khd", grad_scores, query_heads, preferred_element_type=jnp.float32)
        * score_scale
    )
    return (
        attended.reshape(tok_rows, -1),
        grad_query.reshape(tok_rows, -1),
        grad_key.reshape(window_rows, -1),
        grad_value.reshape(window_rows, -1),
    )


def shards(doc_lengths, queries, key_states, value_head_states, out_grad):
    tok_rows = queries.shape[0]
    block_count = REACH + 1
    level_count = block_count.bit_length() - 1
    device_index = lax.axis_index("cp")
    key_value = jnp.stack([key_states, value_head_states])
    window = key_value
    for level_index in range(level_count):
        earlier = from_behind(window, "cp", window.shape[1] // tok_rows)
        window = jnp.concatenate([earlier, window], axis=1)
    query_pos = device_index * tok_rows + lax.iota(jnp.int32, tok_rows)
    key_pos = (device_index - REACH) * tok_rows + lax.iota(jnp.int32, block_count * tok_rows)
    query_ids = document_ids(doc_lengths, query_pos)
    key_ids = document_ids(doc_lengths, key_pos)
    allowed = (query_ids[:, None] == key_ids[None, :]) & (key_pos[None, :] <= query_pos[:, None])
    attended, grad_queries, grad_key, grad_value = attend(queries, window, out_grad, allowed)
    partials = jnp.stack([grad_key, grad_value])
    summed = partials
    for level_index in range(level_count):
        half_width = summed.shape[1] // 2
        later = from_behind(summed[:, :half_width], "cp", -(half_width // tok_rows))
        summed = summed[:, half_width:] + later
    grad_keys = summed[0].astype(jnp.bfloat16)
    grad_values = summed[1].astype(jnp.bfloat16)
    return (attended, grad_queries, grad_keys, grad_values)


def solution(mesh):
    return jax.shard_map(
        shards,
        mesh=mesh,
        in_specs=(
            P("group"),
            P(("group", "cp"), "hd"),
            P(("group", "cp"), "hd"),
            P(("group", "cp"), "hd"),
            P(("group", "cp"), "hd"),
        ),
        out_specs=(
            P(("group", "cp"), "hd"),
            P(("group", "cp"), "hd"),
            P(("group", "cp"), "hd"),
            P(("group", "cp"), "hd"),
        ),
        check_vma=False,
    )
```

profile of v0, /device:TPU:0, one launch (start us, length us, event | category | flops | bytes accessed | tf_op | source)
XLA Modules:
  0.0 83.1 jit_solution(13639317767490587939)
XLA Ops:
  0.6 1.1 %copy.40 = bf16[128,512]{0,1:T(8,128)(2,1)S(1)} copy(bf16[128,512]{1,0:T(8,128)(2,1)} %param.7) | data formatting | bytes 262144 | tf_op args[2]
  1.7 1.0 %copy.41 = bf16[128,512]{0,1:T(8,128)(2,1)S(1)} copy(bf16[128,512]{1,0:T(8,128)(2,1)} %param.8) | data formatting | bytes 262144 | tf_op args[3]
  2.8 4.9 %collective-permute-start = (bf16[2,128,512]{1,2,0:T(8,128)(2,1)S(1)}, bf16[2,128,512]{1,2,0:T(8,128)(2,1)S(1)}, u32[]{:S(2)}, u32[]{:S(2)}) collective-permute-start(bf16[2,128,512]{1,2,0:T(8,128)(2,1)S(1)} %pad_maximum_fusion.1), channel_id=1, source_target_pairs={{0,2},{2,4},{4,6},{6,8},{8,10},{10,12},{12,14},{1,3},{3,5},{5,7},{... | collective-permute-start | bytes 786440 | tf_op jit(solution)/shard_map/ppermute | solution.py:18
  7.7 0.8 reduce-window.8
  8.6 1.3 %copy.45 = bf16[128,2048]{0,1:T(8,128)(2,1)S(1)} copy(bf16[128,2048]{1,0:T(8,128)(2,1)} %param.9) | data formatting | bytes 1048576 | tf_op args[4]
  10.2 3.0 %collective-permute-done = bf16[2,128,512]{1,2,0:T(8,128)(2,1)S(1)} collective-permute-done((bf16[2,128,512]{1,2,0:T(8,128)(2,1)S(1)}, bf16[2,128,512]{1,2,0:T(8,128)(2,1)S(1)}, u32[]{:S(2)}, u32[]{:S(2)}) %collective-permute-start) | collective-permute-done | bytes 262176 | tf_op jit(solution)/shard_map/ppermute | solution.py:18
  13.3 5.4 %collective-permute-start.1 = (bf16[2,256,512]{1,2,0:T(8,128)(2,1)S(1)}, bf16[2,256,512]{1,2,0:T(8,128)(2,1)S(1)}, u32[]{:S(2)}, u32[]{:S(2)}) collective-permute-start(bf16[2,256,512]{1,2,0:T(8,128)(2,1)S(1)} %maximum_maximum_fusion.1), channel_id=1, source_target_pairs={{0,4},{2,6},{4,8},{6,10},{8,12},{10,14},{1,5},{3,7},{5,9},{7,11},{... | collective-permute-start | bytes 1572872 | tf_op jit(solution)/shard_map/ppermute | solution.py:18
  19.0 10.0 %collective-permute-done.1 = bf16[2,256,512]{1,2,0:T(8,128)(2,1)S(1)} collective-permute-done((bf16[2,256,512]{1,2,0:T(8,128)(2,1)S(1)}, bf16[2,256,512]{1,2,0:T(8,128)(2,1)S(1)}, u32[]{:S(2)}, u32[]{:S(2)}) %collective-permute-start.1) | collective-permute-done | bytes 524320 | tf_op jit(solution)/shard_map/ppermute | solution.py:18
  29.2 3.5 %fusion.18 = (f32[4,4,128]{2,1,0:T(4,128)S(1)}, f32[4,4,128,512]{2,3,1,0:T(8,128)}) fusion(pred[128,512]{0,1:T(8,128)(4,1)S(1)} %compare_and_fusion, bf16[512,4,128,1]{0,2,3,1:T(8,128)(2,1)S(1)} %bitcast.90, bf16[128,4,4,128]{0,3,2,1:T(8,128)(2,1)S(1)} %bitcast.84), kind=kOutput, calls=%fused_computation.41 | convolution fusion | flops 272630272 | bytes 5316608 | tf_op jit(solution)/shard_map/sub | solution.py:43
  32.6 2.7 %fusion.7 = bf16[4,4,128,512]{2,3,1,0:T(8,128)(2,1)S(1)} fusion(f32[4,4,128,512]{2,3,1,0:T(8,128)} %get-tuple-element.21, f32[4,4,128]{2,1,0:T(4,128)S(1)} %get-tuple-element.20), kind=kLoop, calls=%fused_computation.13 | loop fusion | flops 2097152 | bytes 6299648 | tf_op jit(solution)/shard_map/convert_element_type | solution.py:45
  35.3 1.3 %multiply_reduce_fusion = (f32[128,4,4]{0,2,1:T(4,128)S(1)}, bf16[4,128,4,128]{3,1,2,0:T(8,128)(2,1)}) fusion(bf16[128,2048]{0,1:T(8,128)(2,1)S(1)} %copy.45, bf16[512,4,128,1]{0,2,3,1:T(8,128)(2,1)S(1)} %bitcast.87, bf16[4,4,128,512]{2,3,1,0:T(8,128)(2,1)S(1)} %fusion.7), kind=kOutput, calls=%fused_computation.23 | convolution fusion | flops 269744128 | bytes 3678208 | tf_op jit(solution)/shard_map/hgqk,khd->qhgd/dot_general | solution.py:46
  36.6 0.8 fusion.19
  37.4 0.3 copy.53
  37.8 3.1 %fusion.2 = bf16[4,4,128,512]{2,3,1,0:T(8,128)(2,1)S(1)} fusion(bf16[512,4,128,1]{0,2,3,1:T(8,128)(2,1)S(1)} %bitcast.88, bf16[128,4,4,128]{0,3,2,1:T(8,128)(2,1)S(1)} %bitcast.81, f32[4,4,128]{2,1,0:T(4,128)S(1)} %bitcast.98, f32[4,4,128,512]{2,3,1,0:T(8,128)} %get-tuple-element.21, f32[4,4,128]{2,1,0:T(4,128)S(1)} %get-tuple-element.20), kind=kOutput, calls=%fused_computation.3 | convolution fusion | flops 272629760 | bytes 7356416 | tf_op jit(solution)/shard_map/qhgd,khd->hgqk/dot_general | solution.py:55
  40.9 0.8 fusion.8
  41.7 0.5 copy-done
  42.7 1.4 %collective-permute-start.2 = (f32[2,256,512]{2,1,0:T(8,128)S(1)}, f32[2,256,512]{2,1,0:T(8,128)S(1)}, u32[]{:S(2)}, u32[]{:S(2)}) collective-permute-start(f32[2,256,512]{2,1,0:T(8,128)S(1)} %pad_maximum_fusion), channel_id=1, source_target_pairs={{4,0},{6,2},{8,4},{10,6},{12,8},{14,10},{5,1},{7,3},{9,5},{11,7},{... | collective-permute-start | bytes 3145736 | tf_op jit(solution)/shard_map/ppermute | solution.py:18
  44.1 24.5 %collective-permute-done.2 = f32[2,256,512]{2,1,0:T(8,128)S(1)} collective-permute-done((f32[2,256,512]{2,1,0:T(8,128)S(1)}, f32[2,256,512]{2,1,0:T(8,128)S(1)}, u32[]{:S(2)}, u32[]{:S(2)}) %collective-permute-start.2) | collective-permute-done | bytes 1048608 | tf_op jit(solution)/shard_map/ppermute | solution.py:18
  68.9 1.4 %collective-permute-start.3 = (f32[2,128,512]{2,1,0:T(8,128)S(1)}, f32[2,128,512]{2,1,0:T(8,128)S(1)}, u32[]{:S(2)}, u32[]{:S(2)}) collective-permute-start(f32[2,128,512]{2,1,0:T(8,128)S(1)} %slice.39), channel_id=1, source_target_pairs={{2,0},{4,2},{6,4},{8,6},{10,8},{12,10},{14,12},{3,1},{5,3},{7,5},{... | collective-permute-start | bytes 1572872 | tf_op jit(solution)/shard_map/ppermute | solution.py:18
  70.4 0.5 fusion.9
  70.9 1.0 %copy.55 = bf16[128,2048]{1,0:T(8,128)(2,1)} copy(bf16[128,2048]{0,1:T(8,128)(2,1)S(1)} %bitcast.89) | data formatting | bytes 1048576
  71.9 1.0 %copy.54 = bf16[128,2048]{1,0:T(8,128)(2,1)} copy(bf16[128,2048]{0,1:T(8,128)(2,1)S(1)} %bitcast.86) | data formatting | bytes 1048576
  72.9 9.4 %collective-permute-done.3 = f32[2,128,512]{2,1,0:T(8,128)S(1)} collective-permute-done((f32[2,128,512]{2,1,0:T(8,128)S(1)}, f32[2,128,512]{2,1,0:T(8,128)S(1)}, u32[]{:S(2)}, u32[]{:S(2)}) %collective-permute-start.3) | collective-permute-done | bytes 524320 | tf_op jit(solution)/shard_map/ppermute | solution.py:18
  82.4 0.7 slice_bitcast_fusion
  (32 shorter events, 1.7 us)
Async XLA Ops:
  0.6 9.3 %copy-start.7 = (bf16[128,2048]{1,0:T(8,128)(2,1)S(1)}, bf16[128,2048]{1,0:T(8,128)(2,1)}, u32[]{:S(2)}) copy-start(bf16[128,2048]{1,0:T(8,128)(2,1)} %param.6) | copy-start | bytes 1572868
  2.8 10.4 %collective-permute-start = (bf16[2,128,512]{1,2,0:T(8,128)(2,1)S(1)}, bf16[2,128,512]{1,2,0:T(8,128)(2,1)S(1)}, u32[]{:S(2)}, u32[]{:S(2)}) collective-permute-start(bf16[2,128,512]{1,2,0:T(8,128)(2,1)S(1)} %pad_maximum_fusion.1), channel_id=1, source_target_pairs={{0,2},{2,4},{4,6},{6,8},{8,10},{10,12},{12,14},{1,3},{3,5},{5,7},{... | collective-permute-start | bytes 786440 | tf_op jit(solution)/shard_map/ppermute | solution.py:18
  10.2 18.9 %copy-start.2 = (bf16[128,2048]{0,1:T(8,128)(2,1)}, bf16[128,2048]{0,1:T(8,128)(2,1)S(1)}, u32[]{:S(2)}) copy-start(bf16[128,2048]{0,1:T(8,128)(2,1)S(1)} %copy.71) | copy-start | bytes 1572868
  13.3 15.7 %collective-permute-start.1 = (bf16[2,256,512]{1,2,0:T(8,128)(2,1)S(1)}, bf16[2,256,512]{1,2,0:T(8,128)(2,1)S(1)}, u32[]{:S(2)}, u32[]{:S(2)}) collective-permute-start(bf16[2,256,512]{1,2,0:T(8,128)(2,1)S(1)} %maximum_maximum_fusion.1), channel_id=1, source_target_pairs={{0,4},{2,6},{4,8},{6,10},{8,12},{10,14},{1,5},{3,7},{5,9},{7,11},{... | collective-permute-start | bytes 1572872 | tf_op jit(solution)/shard_map/ppermute | solution.py:18
  29.1 3.5 %copy-start.5 = (bf16[1,512,512]{1,2,0:T(8,128)(2,1)}, bf16[1,512,512]{1,2,0:T(8,128)(2,1)S(1)}, u32[]{:S(2)}) copy-start(bf16[1,512,512]{1,2,0:T(8,128)(2,1)S(1)} %get-tuple-element.16) | copy-start | bytes 1572868
  37.8 3.1 %copy-start.3 = (bf16[128,2048]{0,1:T(8,128)(2,1)S(1)}, bf16[128,2048]{0,1:T(8,128)(2,1)}, u32[]{:S(2)}) copy-start(bf16[128,2048]{0,1:T(8,128)(2,1)} %copy-done.2) | copy-start | bytes 1572868
  40.9 1.4 %copy-start = (bf16[4,4,128,512]{2,3,1,0:T(8,128)(2,1)}, bf16[4,4,128,512]{2,3,1,0:T(8,128)(2,1)S(1)}, u32[]{:S(2)}) copy-start(bf16[4,4,128,512]{2,3,1,0:T(8,128)(2,1)S(1)} %fusion.2) | copy-start | bytes 6291460
  42.7 27.7 %copy-start.1 = (bf16[4,4,128,512]{2,3,1,0:T(8,128)(2,1)S(1)}, bf16[4,4,128,512]{2,3,1,0:T(8,128)(2,1)}, u32[]{:S(2)}) copy-start(bf16[4,4,128,512]{2,3,1,0:T(8,128)(2,1)} %copy-done) | copy-start | bytes 6291460
  42.7 27.7 %copy-start.6 = (bf16[1,512,512]{1,2,0:T(8,128)(2,1)S(1)}, bf16[1,512,512]{1,2,0:T(8,128)(2,1)}, u32[]{:S(2)}) copy-start(bf16[1,512,512]{1,2,0:T(8,128)(2,1)} %copy-done.5) | copy-start | bytes 1572868
  42.7 26.0 %collective-permute-start.2 = (f32[2,256,512]{2,1,0:T(8,128)S(1)}, f32[2,256,512]{2,1,0:T(8,128)S(1)}, u32[]{:S(2)}, u32[]{:S(2)}) collective-permute-start(f32[2,256,512]{2,1,0:T(8,128)S(1)} %pad_maximum_fusion), channel_id=1, source_target_pairs={{4,0},{6,2},{8,4},{10,6},{12,8},{14,10},{5,1},{7,3},{9,5},{11,7},{... | collective-permute-start | bytes 3145736 | tf_op jit(solution)/shard_map/ppermute | solution.py:18
  68.9 3.0 %copy-start.4 = (bf16[4,128,4,128]{3,1,2,0:T(8,128)(2,1)S(1)}, bf16[4,128,4,128]{3,1,2,0:T(8,128)(2,1)}, u32[]{:S(2)}) copy-start(bf16[4,128,4,128]{3,1,2,0:T(8,128)(2,1)} %get-tuple-element.23) | copy-start | bytes 1572868
  68.9 13.4 %collective-permute-start.3 = (f32[2,128,512]{2,1,0:T(8,128)S(1)}, f32[2,128,512]{2,1,0:T(8,128)S(1)}, u32[]{:S(2)}, u32[]{:S(2)}) collective-permute-start(f32[2,128,512]{2,1,0:T(8,128)S(1)} %slice.39), channel_id=1, source_target_pairs={{2,0},{4,2},{6,4},{8,6},{10,8},{12,10},{14,12},{3,1},{5,3},{7,5},{... | collective-permute-start | bytes 1572872 | tf_op jit(solution)/shard_map/ppermute | solution.py:18
where the time goes:
time: 83.5 us; the launch traced here: 83.1 us
  waiting for transfers between devices  46.9 us (56%)
  starting transfers between devices  13.1 us (16%)
  matrix products  9.95 us (12%)
  local copies, waits for them, and re-layouts  7.74 us (9%)
  other arithmetic  4.47 us (5%)
  between operations  0.93 us (1%)
    ppermute x4, waiting for transfers between devices, from_behind(): return lax.ppermute(value, axis, pairs)  46.9 us
    ppermute x4, starting transfers between devices, from_behind(): return lax.ppermute(value, axis, pairs)  13.1 us
    unnamed x21, local copies, waits for them, and re-layouts  5.98 us
    sub x1, matrix products, attend(): weights_raw = jnp.exp(scores - row_max)  3.46 us
    dot_general x1, matrix products, attend(): jnp.einsum('qhgd,khd->hgqk', grad_heads, value_heads, preferred_element_t...  3.09 us
    convert_element_type x1, other arithmetic, attend(): probs_low = probs.astype(jnp.bfloat16)  2.69 us
  transfers between devices with their start and end apart: 4, of which 4 were waited for; matrix products, arithmetic and copies ran while one was open for 6% of the time, Pallas kernels for 0%

commit v1 on v0

v1 whole, which is shorter than its diff:
```python
import functools
import math

import jax
import jax.numpy as jnp
from jax import lax
from jax.experimental import pallas as pl
from jax.experimental.pallas import tpu as pltpu
from jax.sharding import PartitionSpec as P

HEAD = 128
MASKED = -1e30


def shift(value, by):
    peers = lax.axis_size("cp")
    pairs = [(i, i + by) for i in range(peers) if 0 <= i + by < peers]
    return lax.ppermute(value, "cp", pairs)


def dot(a, b, contract):
    return lax.dot_general(a, b, (contract, ((), ())), preferred_element_type=jnp.float32)


def stacked(block):
    heads = block.shape[1] // HEAD
    return jnp.concatenate([block[:, i * HEAD:(i + 1) * HEAD] for i in range(heads)], axis=0)


def attention_kernel(tok, lens_ref, pos_ref, q_ref, do_ref, k_ref, v_ref, near_ref, mid_ref,
                     o_ref, dq_ref, own_ref, gmid_ref, gnear_ref):
    heads = q_ref.shape[1] // HEAD
    scale = 1.0 / math.sqrt(HEAD)
    start = pos_ref[0]
    query_pos = start + lax.broadcasted_iota(jnp.int32, (1, tok), 1)

    def place(d, carry):
        end, low = carry
        end = end + lens_ref[d]
        return end, jnp.where(end <= query_pos, end, low)

    _, low = lax.fori_loop(0, lens_ref.shape[0], place, (jnp.int32(0), jnp.zeros((1, tok), jnp.int32)))
    low = jnp.concatenate([low - start] * heads, axis=1)
    rel = lax.broadcasted_iota(jnp.int32, (4 * tok, tok * heads), 0) - 3 * tok
    upto = jnp.concatenate([query_pos - start] * heads, axis=1)
    allowed = (rel >= low) & (rel <= upto)

    keys = jnp.concatenate([near_ref[2 * tok:3 * tok], mid_ref[:tok], near_ref[:tok], k_ref[...]], axis=0)
    values = jnp.concatenate([near_ref[3 * tok:], mid_ref[tok:], near_ref[tok:2 * tok], v_ref[...]], axis=0)
    q = stacked(q_ref[...])
    do = stacked(do_ref[...])
    s = dot(keys, q, ((1,), (1,))) * scale
    s = jnp.where(allowed, s, MASKED)
    e = jnp.exp(s - jnp.max(s, axis=0, keepdims=True))
    p = e * (1.0 / jnp.sum(e, axis=0, keepdims=True))
    p_low = p.astype(jnp.bfloat16)
    dp = dot(values, do, ((1,), (1,)))
    delta = jnp.sum(p * dp, axis=0, keepdims=True)
    ds = (p * (dp - delta)).astype(jnp.bfloat16)
    dv = dot(p_low, do, ((1,), (0,)))
    dk = dot(ds, q, ((1,), (0,))) * scale
    gnear_ref[:tok] = dk[2 * tok:3 * tok].astype(gnear_ref.dtype)
    gnear_ref[tok:2 * tok] = dv[2 * tok:3 * tok].astype(gnear_ref.dtype)
    gnear_ref[2 * tok:3 * tok] = dk[:tok].astype(gnear_ref.dtype)
    gnear_ref[3 * tok:] = dv[:tok].astype(gnear_ref.dtype)
    gmid_ref[:tok] = dk[tok:2 * tok]
    gmid_ref[tok:] = dv[tok:2 * tok]
    own_ref[:tok] = dk[3 * tok:]
    own_ref[tok:] = dv[3 * tok:]
    ot = dot(values, p_low, ((0,), (0,)))
    dqt = dot(keys, ds, ((0,), (0,))) * scale
    for i in range(heads):
        o_ref[:, i * HEAD:(i + 1) * HEAD] = ot[:, i * tok:(i + 1) * tok].T.astype(o_ref.dtype)
        dq_ref[:, i * HEAD:(i + 1) * HEAD] = dqt[:, i * tok:(i + 1) * tok].T.astype(dq_ref.dtype)


def attend(doc_lengths, start, queries, out_grad, keys, values, near, mid):
    tok, width = queries.shape
    kv_width = keys.shape[1]
    kv_heads = kv_width // HEAD
    wide = width // kv_heads

    def col(rows, cols):
        return pl.BlockSpec((rows, cols), lambda h: (0, h))

    smem = pl.BlockSpec(memory_space=pltpu.SMEM)
    f32, low = jnp.float32, queries.dtype
    return pl.pallas_call(
        functools.partial(attention_kernel, tok),
        grid=(kv_heads,),
        in_specs=[smem, smem, col(tok, wide), col(tok, wide), col(tok, HEAD), col(tok, HEAD),
                  col(4 * tok, HEAD), col(2 * tok, HEAD)],
        out_specs=[col(tok, wide), col(tok, wide), col(2 * tok, HEAD), col(2 * tok, HEAD), col(4 * tok, HEAD)],
        out_shape=[
            jax.ShapeDtypeStruct((tok, width), low),
            jax.ShapeDtypeStruct((tok, width), low),
            jax.ShapeDtypeStruct((2 * tok, kv_width), f32),
            jax.ShapeDtypeStruct((2 * tok, kv_width), f32),
            jax.ShapeDtypeStruct((4 * tok, kv_width), low),
        ],
        cost_estimate=pl.CostEstimate(
            flops=40 * tok * tok * width, bytes_accessed=8 * tok * width, transcendentals=4 * tok * tok * kv_heads
        ),
    )(doc_lengths, start, queries, out_grad, keys, values, near, mid)


def shards(doc_lengths, queries, key_states, value_head_states, out_grad):
    tok = queries.shape[0]
    start = (lax.axis_index("cp") * tok).astype(jnp.int32).reshape(1)
    own = jnp.concatenate([key_states, value_head_states], axis=0)
    mid = shift(own, 2)
    near = shift(jnp.concatenate([own, mid], axis=0), 1)
    attended, grad_queries, g_own, g_mid, g_near = attend(
        doc_lengths, start, queries, out_grad, key_states, value_head_states, near, mid
    )
    back = shift(g_near, -1).astype(jnp.float32)
    far = shift((g_mid + back[2 * tok:]).astype(g_near.dtype), -2)
    total = (g_own + back[:2 * tok] + far.astype(jnp.float32)).astype(key_states.dtype)
    return attended, grad_queries, total[:tok], total[tok:]


def solution(mesh):
    part = P(("group", "cp"), "hd")
    return jax.shard_map(
        shards,
        mesh=mesh,
        in_specs=(P("group"), part, part, part, part),
        out_specs=(part, part, part, part),
        check_vma=False,
    )
```

time: 83.5 us -> 61.3 us (0.73)
  matrix products: 9.95 us -> 0 us
  waiting for transfers between devices: 46.9 us -> 37.9 us
  Pallas kernels: 0 us -> 7.61 us
  local copies, waits for them, and re-layouts: 7.74 us -> 2.18 us
  other arithmetic: 4.47 us -> 1.42 us
  starting transfers between devices: 13.1 us -> 11.2 us
    ppermute x4, waiting for transfers between devices: 46.9 us -> 37.9 us  [shift(): return lax.ppermute(value, 'cp', pairs)]
    pallas_call x0 -> x1, Pallas kernels: none -> 7.61 us  [attend(): pl.pallas_call(functools.partial(attention_kernel, tok), grid=(kv_heads,)...]
    dot_general x5 -> x0, matrix products: 6.5 us -> none  [the longest x1 3.09 us: attend(): jnp.einsum('qhgd,khd->hgqk', grad_heads, value_heads, preferred_element_t...]
    unnamed x21 -> x12, local copies, waits for them, and re-layouts: 5.98 us -> 1.47 us
    sub x1 -> x0, matrix products: 3.46 us -> none  [attend(): weights_raw = jnp.exp(scores - row_max)]
    convert_element_type x1 -> x3, other arithmetic: 2.69 us -> 0.36 us  [the longest x1 0.14 us: shards(): (g_own + back[:2 * tok] + far.astype(jnp.float32)).astype(key_states.dtype)]
    ppermute x4, starting transfers between devices: 13.1 us -> 11.2 us  [shift(): return lax.ppermute(value, 'cp', pairs)]
    another operation x4 -> x0, other arithmetic: 1.02 us -> none
  transfers between devices with their start and end apart: 4 -> 4, of which waited for: 4 -> 4; matrix products, arithmetic and copies ran while one was open for 6% -> 0% of each run, Pallas kernels for 0% -> 0%
where the time goes in v1:
time: 61.3 us; the launch traced here: 61.1 us
  waiting for transfers between devices  37.9 us (62%)
  starting transfers between devices  11.2 us (18%)
  Pallas kernels  7.61 us (12%)
  local copies, waits for them, and re-layouts  2.18 us (4%)
  other arithmetic  1.42 us (2%)
  between operations  0.74 us (1%)
    ppermute x4, waiting for transfers between devices, shift(): return lax.ppermute(value, 'cp', pairs)  37.9 us
    ppermute x4, starting transfers between devices, shift(): return lax.ppermute(value, 'cp', pairs)  11.2 us
    pallas_call x1, Pallas kernels, attend(): pl.pallas_call(functools.partial(attention_kernel, tok), grid=(kv_heads,)...  7.61 us
    unnamed x12, local copies, waits for them, and re-layouts  1.47 us
  transfers between devices with their start and end apart: 4, of which 4 were waited for; matrix products, arithmetic and copies ran while one was open for 0% of the time, Pallas kernels for 0%

profile of v1, /device:TPU:0, one launch (start us, length us, event | category | flops | bytes accessed | tf_op | source)
XLA Modules:
  0.0 61.1 jit_solution(3341254584494649291)
XLA Ops:
  0.6 0.0 copy-start.3
  0.6 0.0 copy-start.2
  0.7 1.0 %pad_maximum_fusion.1 = bf16[256,512]{1,0:T(8,128)(2,1)S(1)} fusion(bf16[128,512]{1,0:T(8,128)(2,1)} %v_ref.1, bf16[128,512]{1,0:T(8,128)(2,1)} %k_ref.1), kind=kLoop, calls=%fused_computation.6 | loop fusion | flops 524288 | bytes 524288 | tf_op jit(solution)/shard_map/concatenate | solution.py:110
  1.7 5.0 %collective-permute-start = (bf16[256,512]{1,0:T(8,128)(2,1)S(1)}, bf16[256,512]{1,0:T(8,128)(2,1)S(1)}, u32[]{:S(2)}, u32[]{:S(2)}) collective-permute-start(bf16[256,512]{1,0:T(8,128)(2,1)S(1)} %pad_maximum_fusion.1), channel_id=1, source_target_pairs={{0,4},{2,6},{4,8},{6,10},{8,12},{10,14},{1,5},{3,7},{5,9},{7,11},{... | collective-permute-start | bytes 786440 | tf_op jit(solution)/shard_map/ppermute | solution.py:18
  6.7 5.5 %collective-permute-done.mid_ref = bf16[256,512]{1,0:T(8,128)(2,1)S(1)} collective-permute-done((bf16[256,512]{1,0:T(8,128)(2,1)S(1)}, bf16[256,512]{1,0:T(8,128)(2,1)S(1)}, u32[]{:S(2)}, u32[]{:S(2)}) %collective-permute-start) | collective-permute-done | bytes 262176 | tf_op jit(solution)/shard_map/ppermute | solution.py:18
  12.2 0.0 copy-done.3
  12.2 0.0 copy-done.2
  12.2 0.7 %copy-done.4 = bf16[256,512]{1,0:T(8,128)(2,1)} copy-done((bf16[256,512]{1,0:T(8,128)(2,1)}, bf16[256,512]{1,0:T(8,128)(2,1)S(1)}, u32[]{:S(2)}) %copy-start.4) | copy-done | bytes 262168
  12.9 3.4 %collective-permute-start.1 = (bf16[512,512]{1,0:T(8,128)(2,1)S(1)}, bf16[512,512]{1,0:T(8,128)(2,1)S(1)}, u32[]{:S(2)}, u32[]{:S(2)}) collective-permute-start(bf16[512,512]{1,0:T(8,128)(2,1)S(1)} %pad_maximum_fusion), channel_id=1, source_target_pairs={{0,2},{2,4},{4,6},{6,8},{8,10},{10,12},{12,14},{1,3},{3,5},{5,7},{... | collective-permute-start | bytes 1572872 | tf_op jit(solution)/shard_map/ppermute | solution.py:18
  16.3 10.3 %collective-permute-done.1.near_ref = bf16[512,512]{1,0:T(8,128)(2,1)S(1)} collective-permute-done((bf16[512,512]{1,0:T(8,128)(2,1)S(1)}, bf16[512,512]{1,0:T(8,128)(2,1)S(1)}, u32[]{:S(2)}, u32[]{:S(2)}) %collective-permute-start.1) | collective-permute-done | bytes 524320 | tf_op jit(solution)/shard_map/ppermute | solution.py:18
  26.6 0.8 %copy-done.5 = bf16[512,512]{1,0:T(8,128)(2,1)} copy-done((bf16[512,512]{1,0:T(8,128)(2,1)}, bf16[512,512]{1,0:T(8,128)(2,1)S(1)}, u32[]{:S(2)}) %copy-start.5) | copy-done | bytes 524312
  27.4 7.6 %shard_map.84 = (bf16[128,2048]{1,0:T(8,128)(2,1)}, bf16[128,2048]{1,0:T(8,128)(2,1)}, f32[256,512]{1,0:T(8,128)}, f32[256,512]{1,0:T(8,128)}, bf16[512,512]{1,0:T(8,128)(2,1)}) custom-call(s32[4]{0:T(128)} %lens_ref.1, s32[1]{0:T(128)} %bitcast.pos_ref, bf16[128,2048]{1,0:T(8,128)(2,1)} %q_ref.1, bf16[128,2048]{1,0:T(8,128)(2,1)} %do_ref.1, ...), custom_call_target="tpu_custom_call" | custom-call | flops 1342177280 | bytes 2097152 | tf_op jit(solution)/shard_map/pallas_call | solution.py:88
  35.0 0.0 copy-start.1
  35.0 1.4 %collective-permute-start.2 = (bf16[512,512]{1,0:T(8,128)(2,1)}, bf16[512,512]{1,0:T(8,128)(2,1)S(1)}, u32[]{:S(2)}, u32[]{:S(2)}) collective-permute-start(bf16[512,512]{1,0:T(8,128)(2,1)} %get-tuple-element.12), channel_id=1, source_target_pairs={{2,0},{4,2},{6,4},{8,6},{10,8},{12,10},{14,12},{3,1},{5,3},{7,5},{... | collective-permute-start | bytes 1572872 | tf_op jit(solution)/shard_map/ppermute | solution.py:18
  36.4 13.5 %collective-permute-done.2 = bf16[512,512]{1,0:T(8,128)(2,1)S(1)} collective-permute-done((bf16[512,512]{1,0:T(8,128)(2,1)}, bf16[512,512]{1,0:T(8,128)(2,1)S(1)}, u32[]{:S(2)}, u32[]{:S(2)}) %collective-permute-start.2) | collective-permute-done | bytes 524320 | tf_op jit(solution)/shard_map/ppermute | solution.py:18
  50.0 0.1 convert_element_type.12
  50.1 0.0 copy-done.1
  50.1 0.0 copy-start
  50.1 0.1 fusion
  50.2 1.4 %collective-permute-start.3 = (bf16[256,512]{1,0:T(8,128)(2,1)S(1)}, bf16[256,512]{1,0:T(8,128)(2,1)S(1)}, u32[]{:S(2)}, u32[]{:S(2)}) collective-permute-start(bf16[256,512]{1,0:T(8,128)(2,1)S(1)} %fusion), channel_id=1, source_target_pairs={{4,0},{6,2},{8,4},{10,6},{12,8},{14,10},{5,1},{7,3},{9,5},{11,7},{... | collective-permute-start | bytes 786440 | tf_op jit(solution)/shard_map/ppermute | solution.py:18
  51.6 8.6 %collective-permute-done.3 = bf16[256,512]{1,0:T(8,128)(2,1)S(1)} collective-permute-done((bf16[256,512]{1,0:T(8,128)(2,1)S(1)}, bf16[256,512]{1,0:T(8,128)(2,1)S(1)}, u32[]{:S(2)}, u32[]{:S(2)}) %collective-permute-start.3) | collective-permute-done | bytes 262176 | tf_op jit(solution)/shard_map/ppermute | solution.py:18
  60.2 0.0 copy-done
  60.2 0.1 fusion.2
  60.4 0.7 %fusion.3 = (bf16[128,512]{1,0:T(8,128)(2,1)}, bf16[128,512]{1,0:T(8,128)(2,1)}) fusion(bf16[256,512]{1,0:T(8,128)(2,1)S(1)} %fusion.2), kind=kLoop, calls=%fused_computation.7 | loop fusion | bytes 524288 | tf_op jit(solution)/shard_map/slice | solution.py:119
  (3 shorter events, 0.0 us)
Async XLA Ops:
  0.6 11.6 %copy-start.3 = (bf16[128,512]{1,0:T(8,128)(2,1)S(1)}, bf16[128,512]{1,0:T(8,128)(2,1)}, u32[]{:S(2)}) copy-start(bf16[128,512]{1,0:T(8,128)(2,1)} %v_ref.1) | copy-start | bytes 393220
  0.6 11.6 %copy-start.2 = (bf16[128,512]{1,0:T(8,128)(2,1)S(1)}, bf16[128,512]{1,0:T(8,128)(2,1)}, u32[]{:S(2)}) copy-start(bf16[128,512]{1,0:T(8,128)(2,1)} %k_ref.1) | copy-start | bytes 393220
  1.7 10.5 %collective-permute-start = (bf16[256,512]{1,0:T(8,128)(2,1)S(1)}, bf16[256,512]{1,0:T(8,128)(2,1)S(1)}, u32[]{:S(2)}, u32[]{:S(2)}) collective-permute-start(bf16[256,512]{1,0:T(8,128)(2,1)S(1)} %pad_maximum_fusion.1), channel_id=1, source_target_pairs={{0,4},{2,6},{4,8},{6,10},{8,12},{10,14},{1,5},{3,7},{5,9},{7,11},{... | collective-permute-start | bytes 786440 | tf_op jit(solution)/shard_map/ppermute | solution.py:18
  12.2 0.7 %copy-start.4 = (bf16[256,512]{1,0:T(8,128)(2,1)}, bf16[256,512]{1,0:T(8,128)(2,1)S(1)}, u32[]{:S(2)}) copy-start(bf16[256,512]{1,0:T(8,128)(2,1)S(1)} %collective-permute-done.mid_ref) | copy-start | bytes 786436
  12.9 13.7 %collective-permute-start.1 = (bf16[512,512]{1,0:T(8,128)(2,1)S(1)}, bf16[512,512]{1,0:T(8,128)(2,1)S(1)}, u32[]{:S(2)}, u32[]{:S(2)}) collective-permute-start(bf16[512,512]{1,0:T(8,128)(2,1)S(1)} %pad_maximum_fusion), channel_id=1, source_target_pairs={{0,2},{2,4},{4,6},{6,8},{8,10},{10,12},{12,14},{1,3},{3,5},{5,7},{... | collective-permute-start | bytes 1572872 | tf_op jit(solution)/shard_map/ppermute | solution.py:18
  26.6 0.8 %copy-start.5 = (bf16[512,512]{1,0:T(8,128)(2,1)}, bf16[512,512]{1,0:T(8,128)(2,1)S(1)}, u32[]{:S(2)}) copy-start(bf16[512,512]{1,0:T(8,128)(2,1)S(1)} %collective-permute-done.1.near_ref) | copy-start | bytes 1572868
  35.0 15.1 %copy-start.1 = (f32[256,512]{1,0:T(8,128)S(1)}, f32[256,512]{1,0:T(8,128)}, u32[]{:S(2)}) copy-start(f32[256,512]{1,0:T(8,128)} %get-tuple-element.13) | copy-start | bytes 1572868
  35.0 14.9 %collective-permute-start.2 = (bf16[512,512]{1,0:T(8,128)(2,1)}, bf16[512,512]{1,0:T(8,128)(2,1)S(1)}, u32[]{:S(2)}, u32[]{:S(2)}) collective-permute-start(bf16[512,512]{1,0:T(8,128)(2,1)} %get-tuple-element.12), channel_id=1, source_target_pairs={{2,0},{4,2},{6,4},{8,6},{10,8},{12,10},{14,12},{3,1},{5,3},{7,5},{... | collective-permute-start | bytes 1572872 | tf_op jit(solution)/shard_map/ppermute | solution.py:18
  50.1 10.1 %copy-start = (f32[256,512]{1,0:T(8,128)S(1)}, f32[256,512]{1,0:T(8,128)}, u32[]{:S(2)}) copy-start(f32[256,512]{1,0:T(8,128)} %get-tuple-element.11) | copy-start | bytes 1572868
  50.2 10.0 %collective-permute-start.3 = (bf16[256,512]{1,0:T(8,128)(2,1)S(1)}, bf16[256,512]{1,0:T(8,128)(2,1)S(1)}, u32[]{:S(2)}, u32[]{:S(2)}) collective-permute-start(bf16[256,512]{1,0:T(8,128)(2,1)S(1)} %fusion), channel_id=1, source_target_pairs={{4,0},{6,2},{8,4},{10,6},{12,8},{14,10},{5,1},{7,3},{9,5},{11,7},{... | collective-permute-start | bytes 786440 | tf_op jit(solution)/shard_map/ppermute | solution.py:18

commit v2 on v1

--- a/solution.py
+++ b/solution.py
@@ -14,8 +14,7 @@
 
 def shift(value, by):
     peers = lax.axis_size("cp")
-    pairs = [(i, i + by) for i in range(peers) if 0 <= i + by < peers]
-    return lax.ppermute(value, "cp", pairs)
+    return lax.ppermute(value, "cp", [(i, (i + by) % peers) for i in range(peers)])
 
 
 def dot(a, b, contract):
@@ -27,8 +26,8 @@
     return jnp.concatenate([block[:, i * HEAD:(i + 1) * HEAD] for i in range(heads)], axis=0)
 
 
-def attention_kernel(tok, lens_ref, pos_ref, q_ref, do_ref, k_ref, v_ref, near_ref, mid_ref,
-                     o_ref, dq_ref, own_ref, gmid_ref, gnear_ref):
+def attention_kernel(tok, lens_ref, pos_ref, q_ref, do_ref, k_ref, v_ref, near_ref, mid_ref, *rest):
+    o_ref, dq_ref, own_ref, gmid_ref, gnear_ref = rest[-5:]
     heads = q_ref.shape[1] // HEAD
     scale = 1.0 / math.sqrt(HEAD)
     start = pos_ref[0]
@@ -74,23 +73,25 @@
         dq_ref[:, i * HEAD:(i + 1) * HEAD] = dqt[:, i * tok:(i + 1) * tok].T.astype(dq_ref.dtype)
 
 
-def attend(doc_lengths, start, queries, out_grad, keys, values, near, mid):
+def attend(doc_lengths, start, queries, out_grad, keys, values, near, mid, first, done):
     tok, width = queries.shape
-    kv_width = keys.shape[1]
-    kv_heads = kv_width // HEAD
-    wide = width // kv_heads
+    kv_heads = near.shape[1] // HEAD
+    wide = width // (keys.shape[1] // HEAD)
 
-    def col(rows, cols):
-        return pl.BlockSpec((rows, cols), lambda h: (0, h))
+    def col(rows, cols, offset=0):
+        return pl.BlockSpec((rows, cols), lambda h: (0, h + offset))
 
     smem = pl.BlockSpec(memory_space=pltpu.SMEM)
     f32, low = jnp.float32, queries.dtype
+    kv_width = kv_heads * HEAD
     return pl.pallas_call(
         functools.partial(attention_kernel, tok),
         grid=(kv_heads,),
-        in_specs=[smem, smem, col(tok, wide), col(tok, wide), col(tok, HEAD), col(tok, HEAD),
-                  col(4 * tok, HEAD), col(2 * tok, HEAD)],
-        out_specs=[col(tok, wide), col(tok, wide), col(2 * tok, HEAD), col(2 * tok, HEAD), col(4 * tok, HEAD)],
+        in_specs=[smem, smem, col(tok, wide, first), col(tok, wide, first), col(tok, HEAD, first),
+                  col(tok, HEAD, first), col(4 * tok, HEAD), col(2 * tok, HEAD)]
+        + [pl.BlockSpec(memory_space=pl.ANY)] * len(done),
+        out_specs=[col(tok, wide, first), col(tok, wide, first), col(2 * tok, HEAD), col(2 * tok, HEAD),
+                   col(4 * tok, HEAD)],
         out_shape=[
             jax.ShapeDtypeStruct((tok, width), low),
             jax.ShapeDtypeStruct((tok, width), low),
@@ -98,25 +99,38 @@
             jax.ShapeDtypeStruct((2 * tok, kv_width), f32),
             jax.ShapeDtypeStruct((4 * tok, kv_width), low),
         ],
+        input_output_aliases={8 + i: i for i in range(len(done))},
+        compiler_params=pltpu.CompilerParams(vmem_limit_bytes=24 * 1024 * 1024),
         cost_estimate=pl.CostEstimate(
-            flops=40 * tok * tok * width, bytes_accessed=8 * tok * width, transcendentals=4 * tok * tok * kv_heads
+            flops=160 * tok * tok * wide * kv_heads, bytes_accessed=8 * tok * width, transcendentals=0
         ),
-    )(doc_lengths, start, queries, out_grad, keys, values, near, mid)
+    )(doc_lengths, start, queries, out_grad, keys, values, near, mid, *done)
 
 
 def shards(doc_lengths, queries, key_states, value_head_states, out_grad):
     tok = queries.shape[0]
     start = (lax.axis_index("cp") * tok).astype(jnp.int32).reshape(1)
-    own = jnp.concatenate([key_states, value_head_states], axis=0)
-    mid = shift(own, 2)
-    near = shift(jnp.concatenate([own, mid], axis=0), 1)
-    attended, grad_queries, g_own, g_mid, g_near = attend(
-        doc_lengths, start, queries, out_grad, key_states, value_head_states, near, mid
-    )
-    back = shift(g_near, -1).astype(jnp.float32)
-    far = shift((g_mid + back[2 * tok:]).astype(g_near.dtype), -2)
-    total = (g_own + back[:2 * tok] + far.astype(jnp.float32)).astype(key_states.dtype)
-    return attended, grad_queries, total[:tok], total[tok:]
+    firsts = range(key_states.shape[1] // HEAD)
+    cols = [slice(f * HEAD, (f + 1) * HEAD) for f in firsts]
+    own = [jnp.concatenate([key_states[:, c], value_head_states[:, c]], axis=0) for c in cols]
+    mid = [shift(o, 2) for o in own]
+    near = [shift(jnp.concatenate([o, m], axis=0), 1) for o, m in zip(own, mid)]
+    done = ()
+    partial = []
+    for i, f in enumerate(firsts):
+        *done, g_own, g_mid, g_near = attend(
+            doc_lengths, start, queries, out_grad, key_states, value_head_states, near[i], mid[i], f, done
+        )
+        partial.append((g_own, g_mid, g_near))
+    total = []
+    backs = [shift(g_near, -1).astype(jnp.float32) for _, _, g_near in partial]
+    fars = [shift((g_mid + b[2 * tok:]).astype(g_near.dtype), -2) for (_, g_mid, g_near), b in zip(partial, backs)]
+    total = [
+        (g_own + b[:2 * tok] + far.astype(jnp.float32)).astype(key_states.dtype)
+        for (g_own, _, _), b, far in zip(partial, backs, fars)
+    ]
+    total = jnp.concatenate(total, axis=1)
+    return *done, total[:tok], total[tok:]
 
 
 def solution(mesh):

time: 61.3 us -> 43.7 us (0.71)
  waiting for transfers between devices: 37.9 us -> 7.22 us
  starting transfers between devices: 11.2 us -> 23 us
  Pallas kernels: 7.61 us -> 10.5 us
  other arithmetic: 1.42 us -> 0.33 us
    ppermute x4 -> x16, waiting for transfers between devices: 37.9 us -> 7.22 us  [shift(): lax.ppermute(value, 'cp', [(i, (i + by) % peers) for i in range(peers)])]
    ppermute x4 -> x16, starting transfers between devices: 11.2 us -> 23 us  [shift(): lax.ppermute(value, 'cp', [(i, (i + by) % peers) for i in range(peers)])]
    pallas_call x1 -> x4, Pallas kernels: 7.61 us -> 10.5 us  [attend(): pl.pallas_call(functools.partial(attention_kernel, tok), grid=(kv_heads,)...]
    unnamed x12 -> x10, local copies, waits for them, and re-layouts: 1.47 us -> 0.03 us
    concatenate x2 -> x9, other arithmetic: 1.06 us -> 0.09 us  [the longest x4 0.04 us: shards(): near = [shift(jnp.concatenate([o, m], axis=0), 1) for o, m in zip(own, mid)]]
    slice x1 -> x2, local copies, waits for them, and re-layouts: 0.72 us -> 1.62 us  [the longest x1 0.9 us: shards(): key_states[:, c]]
  transfers between devices with their start and end apart: 4 -> 16, of which waited for: 4 -> 7; matrix products, arithmetic and copies ran while one was open for 0% -> 1% of each run, Pallas kernels for 0% -> 24%
where the time goes in v2:
time: 43.7 us; the launch traced here: 43.5 us
  starting transfers between devices  23 us (53%)
  Pallas kernels  10.5 us (24%)
  waiting for transfers between devices  7.22 us (17%)
  local copies, waits for them, and re-layouts  1.64 us (4%)
  between operations  0.79 us (2%)
    ppermute x16, starting transfers between devices, shift(): lax.ppermute(value, 'cp', [(i, (i + by) % peers) for i in range(peers)])  23 us
    pallas_call x4, Pallas kernels, attend(): pl.pallas_call(functools.partial(attention_kernel, tok), grid=(kv_heads,)...  10.5 us
    ppermute x16, waiting for transfers between devices, shift(): lax.ppermute(value, 'cp', [(i, (i + by) % peers) for i in range(peers)])  7.22 us
    slice x1, local copies, waits for them, and re-layouts, shards(): key_states[:, c]  0.9 us
  transfers between devices with their start and end apart: 16, of which 7 were waited for; matrix products, arithmetic and copies ran while one was open for 1% of the time, Pallas kernels for 24%

profile of v2, /device:TPU:0, one launch (start us, length us, event | category | flops | bytes accessed | tf_op | source)
XLA Modules:
  0.0 43.5 jit_solution(4183559678347010928)
XLA Ops:
  0.6 0.9 %fusion.13 = (bf16[128,128]{1,0:T(8,128)(2,1)S(1)}, bf16[128,128]{1,0:T(8,128)(2,1)S(1)}, bf16[128,128]{1,0:T(8,128)(2,1)S(1)}, bf16[128,128]{1,0:T(8,128)(2,1)S...) fusion(bf16[128,512]{1,0:T(8,128)(2,1)} %k_ref.7, ...), kind=kLoop, calls=%fused_computation.30 | loop fusion | bytes 524288 | tf_op jit(solution)/shard_map/slice | solution.py:115
  1.5 3.1 %collective-permute-start.6 = (bf16[256,128]{1,0:T(8,128)(2,1)S(1)}, bf16[256,128]{1,0:T(8,128)(2,1)S(1)}, u32[]{:S(2)}, u32[]{:S(2)}) collective-permute-start(bf16[256,128]{1,0:T(8,128)(2,1)S(1)} %pad_maximum_fusion.8), channel_id=1, source_target_pairs={{0,4},{2,6},{4,8},{6,10},{8,12},{10,14},{12,0},{14,2},{1,5},{3,7},... | collective-permute-start | bytes 196616 | tf_op jit(solution)/shard_map/ppermute | solution.py:17
  4.7 1.6 %collective-permute-start.4 = (bf16[256,128]{1,0:T(8,128)(2,1)S(1)}, bf16[256,128]{1,0:T(8,128)(2,1)S(1)}, u32[]{:S(2)}, u32[]{:S(2)}) collective-permute-start(bf16[256,128]{1,0:T(8,128)(2,1)S(1)} %pad_maximum_fusion.7), channel_id=1, source_target_pairs={{0,4},{2,6},{4,8},{6,10},{8,12},{10,14},{12,0},{14,2},{1,5},{3,7},... | collective-permute-start | bytes 196616 | tf_op jit(solution)/shard_map/ppermute | solution.py:17
  6.2 1.6 %collective-permute-start.2 = (bf16[256,128]{1,0:T(8,128)(2,1)S(1)}, bf16[256,128]{1,0:T(8,128)(2,1)S(1)}, u32[]{:S(2)}, u32[]{:S(2)}) collective-permute-start(bf16[256,128]{1,0:T(8,128)(2,1)S(1)} %pad_maximum_fusion.6), channel_id=1, source_target_pairs={{0,4},{2,6},{4,8},{6,10},{8,12},{10,14},{12,0},{14,2},{1,5},{3,7},... | collective-permute-start | bytes 196616 | tf_op jit(solution)/shard_map/ppermute | solution.py:17
  8.0 1.3 %collective-permute-done.6.mid_ref = bf16[256,128]{1,0:T(8,128)(2,1)S(1)} collective-permute-done((bf16[256,128]{1,0:T(8,128)(2,1)S(1)}, bf16[256,128]{1,0:T(8,128)(2,1)S(1)}, u32[]{:S(2)}, u32[]{:S(2)}) %collective-permute-start.6) | collective-permute-done | bytes 65568 | tf_op jit(solution)/shard_map/ppermute | solution.py:17
  9.3 2.0 %collective-permute-start.7 = (bf16[512,128]{1,0:T(8,128)(2,1)S(1)}, bf16[512,128]{1,0:T(8,128)(2,1)S(1)}, u32[]{:S(2)}, u32[]{:S(2)}) collective-permute-start(bf16[512,128]{1,0:T(8,128)(2,1)S(1)} %pad_maximum_fusion.4), channel_id=1, source_target_pairs={{0,2},{2,4},{4,6},{6,8},{8,10},{10,12},{12,14},{14,0},{1,3},{3,5},... | collective-permute-start | bytes 393224 | tf_op jit(solution)/shard_map/ppermute | solution.py:17
  11.4 1.5 %collective-permute-start.5 = (bf16[512,128]{1,0:T(8,128)(2,1)S(1)}, bf16[512,128]{1,0:T(8,128)(2,1)S(1)}, u32[]{:S(2)}, u32[]{:S(2)}) collective-permute-start(bf16[512,128]{1,0:T(8,128)(2,1)S(1)} %pad_maximum_fusion.3), channel_id=1, source_target_pairs={{0,2},{2,4},{4,6},{6,8},{8,10},{10,12},{12,14},{14,0},{1,3},{3,5},... | collective-permute-start | bytes 393224 | tf_op jit(solution)/shard_map/ppermute | solution.py:17
  13.0 1.6 %collective-permute-start.3 = (bf16[512,128]{1,0:T(8,128)(2,1)S(1)}, bf16[512,128]{1,0:T(8,128)(2,1)S(1)}, u32[]{:S(2)}, u32[]{:S(2)}) collective-permute-start(bf16[512,128]{1,0:T(8,128)(2,1)S(1)} %pad_maximum_fusion.2), channel_id=1, source_target_pairs={{0,2},{2,4},{4,6},{6,8},{8,10},{10,12},{12,14},{14,0},{1,3},{3,5},... | collective-permute-start | bytes 393224 | tf_op jit(solution)/shard_map/ppermute | solution.py:17
  14.7 1.5 %collective-permute-start.1 = (bf16[512,128]{1,0:T(8,128)(2,1)S(1)}, bf16[512,128]{1,0:T(8,128)(2,1)S(1)}, u32[]{:S(2)}, u32[]{:S(2)}) collective-permute-start(bf16[512,128]{1,0:T(8,128)(2,1)S(1)} %pad_maximum_fusion.1), channel_id=1, source_target_pairs={{0,2},{2,4},{4,6},{6,8},{8,10},{10,12},{12,14},{14,0},{1,3},{3,5},... | collective-permute-start | bytes 393224 | tf_op jit(solution)/shard_map/ppermute | solution.py:17
  16.2 2.2 %collective-permute-done.7.near_ref = bf16[512,128]{1,0:T(8,128)(2,1)S(1)} collective-permute-done((bf16[512,128]{1,0:T(8,128)(2,1)S(1)}, bf16[512,128]{1,0:T(8,128)(2,1)S(1)}, u32[]{:S(2)}, u32[]{:S(2)}) %collective-permute-start.7) | collective-permute-done | bytes 131104 | tf_op jit(solution)/shard_map/ppermute | solution.py:17
  18.4 2.6 %shard_map.84 = (bf16[128,2048]{1,0:T(8,128)(2,1)}, bf16[128,2048]{1,0:T(8,128)(2,1)}, f32[256,128]{1,0:T(8,128)S(1)}, f32[256,128]{1,0:T(8,128)S(1)}, bf16[512,128]{1,0:T(8,128)(2,1)S(1)}) custom-call(s32[4]{0:T(128)S(1)} %copy-done.4, s32[1]{0:T(128)} %bitcast.pos_ref, bf16[128,2048]{1,0:T(8,128)(2,1)S(1)} %copy-done.2, bf16[128,2048]{1,0:T(8,128)(2,1)S(1)} %copy-done.3, ...), custom_call_target="tpu_custom_call" | custom-call | flops 1342177280 | bytes 2097152 | tf_op jit(solution)/shard_map/pallas_call | solution.py:87
  21.0 1.1 %collective-permute-start.8 = (bf16[512,128]{1,0:T(8,128)(2,1)S(1)}, bf16[512,128]{1,0:T(8,128)(2,1)S(1)}, u32[]{:S(2)}, u32[]{:S(2)}) collective-permute-start(bf16[512,128]{1,0:T(8,128)(2,1)S(1)} %get-tuple-element.33), channel_id=1, source_target_pairs={{0,14},{2,0},{4,2},{6,4},{8,6},{10,8},{12,10},{14,12},{1,15},{3,1}... | collective-permute-start | bytes 393224 | tf_op jit(solution)/shard_map/ppermute | solution.py:17
  22.1 2.6 %shard_map.85 = (bf16[128,2048]{1,0:T(8,128)(2,1)}, bf16[128,2048]{1,0:T(8,128)(2,1)}, f32[256,128]{1,0:T(8,128)S(1)}, f32[256,128]{1,0:T(8,128)S(1)}, bf16[512,128]{1,0:T(8,128)(2,1)S(1)}) custom-call(s32[4]{0:T(128)S(1)} %copy-done.4, s32[1]{0:T(128)} %bitcast.pos_ref, ...), custom_call_target="tpu_custom_call", output_to_operand_aliasing={{0}: (8, {}), {1}: (9, {})} | custom-call | flops 1342177280 | bytes 2097152 | tf_op jit(solution)/shard_map/pallas_call | solution.py:87
  24.8 1.6 %collective-permute-start.10 = (bf16[512,128]{1,0:T(8,128)(2,1)S(1)}, bf16[512,128]{1,0:T(8,128)(2,1)S(1)}, u32[]{:S(2)}, u32[]{:S(2)}) collective-permute-start(bf16[512,128]{1,0:T(8,128)(2,1)S(1)} %get-tuple-element.36), channel_id=1, source_target_pairs={{0,14},{2,0},{4,2},{6,4},{8,6},{10,8},{12,10},{14,12},{1,15},{3,1}... | collective-permute-start | bytes 393224 | tf_op jit(solution)/shard_map/ppermute | solution.py:17
  26.4 2.6 %shard_map.86 = (bf16[128,2048]{1,0:T(8,128)(2,1)}, bf16[128,2048]{1,0:T(8,128)(2,1)}, f32[256,128]{1,0:T(8,128)S(1)}, f32[256,128]{1,0:T(8,128)S(1)}, bf16[512,128]{1,0:T(8,128)(2,1)S(1)}) custom-call(s32[4]{0:T(128)S(1)} %copy-done.4, s32[1]{0:T(128)} %bitcast.pos_ref, ...), custom_call_target="tpu_custom_call", output_to_operand_aliasing={{0}: (8, {}), {1}: (9, {})} | custom-call | flops 1342177280 | bytes 2097152 | tf_op jit(solution)/shard_map/pallas_call | solution.py:87
  29.3 2.6 %shard_map.87 = (bf16[128,2048]{1,0:T(8,128)(2,1)}, bf16[128,2048]{1,0:T(8,128)(2,1)}, f32[256,128]{1,0:T(8,128)S(1)}, f32[256,128]{1,0:T(8,128)S(1)}, bf16[512,128]{1,0:T(8,128)(2,1)S(1)}) custom-call(s32[4]{0:T(128)S(1)} %copy-done.4, s32[1]{0:T(128)} %bitcast.pos_ref, ...), custom_call_target="tpu_custom_call", output_to_operand_aliasing={{0}: (8, {}), {1}: (9, {})} | custom-call | flops 1342177280 | bytes 2097152 | tf_op jit(solution)/shard_map/pallas_call | solution.py:87
  31.9 1.8 %collective-permute-start.14 = (bf16[512,128]{1,0:T(8,128)(2,1)S(1)}, bf16[512,128]{1,0:T(8,128)(2,1)S(1)}, u32[]{:S(2)}, u32[]{:S(2)}) collective-permute-start(bf16[512,128]{1,0:T(8,128)(2,1)S(1)} %get-tuple-element.42), channel_id=1, source_target_pairs={{0,14},{2,0},{4,2},{6,4},{8,6},{10,8},{12,10},{14,12},{1,15},{3,1}... | collective-permute-start | bytes 393224 | tf_op jit(solution)/shard_map/ppermute | solution.py:17
  33.8 0.7 %collective-permute-start.9 = (bf16[256,128]{1,0:T(8,128)(2,1)S(1)}, bf16[256,128]{1,0:T(8,128)(2,1)S(1)}, u32[]{:S(2)}, u32[]{:S(2)}) collective-permute-start(bf16[256,128]{1,0:T(8,128)(2,1)S(1)} %fusion.9), channel_id=1, source_target_pairs={{0,12},{2,14},{4,0},{6,2},{8,4},{10,6},{12,8},{14,10},{1,13},{3,15... | collective-permute-start | bytes 196616 | tf_op jit(solution)/shard_map/ppermute | solution.py:17
  34.6 2.5 %collective-permute-start.11 = (bf16[256,128]{1,0:T(8,128)(2,1)S(1)}, bf16[256,128]{1,0:T(8,128)(2,1)S(1)}, u32[]{:S(2)}, u32[]{:S(2)}) collective-permute-start(bf16[256,128]{1,0:T(8,128)(2,1)S(1)} %fusion.6), channel_id=1, source_target_pairs={{0,12},{2,14},{4,0},{6,2},{8,4},{10,6},{12,8},{14,10},{1,13},{3,15... | collective-permute-start | bytes 196616 | tf_op jit(solution)/shard_map/ppermute | solution.py:17
  37.1 1.3 %collective-permute-start.13 = (bf16[256,128]{1,0:T(8,128)(2,1)S(1)}, bf16[256,128]{1,0:T(8,128)(2,1)S(1)}, u32[]{:S(2)}, u32[]{:S(2)}) collective-permute-start(bf16[256,128]{1,0:T(8,128)(2,1)S(1)} %fusion.3), channel_id=1, source_target_pairs={{0,12},{2,14},{4,0},{6,2},{8,4},{10,6},{12,8},{14,10},{1,13},{3,15... | collective-permute-start | bytes 196616 | tf_op jit(solution)/shard_map/ppermute | solution.py:17
  38.4 0.7 %collective-permute-start.15 = (bf16[256,128]{1,0:T(8,128)(2,1)S(1)}, bf16[256,128]{1,0:T(8,128)(2,1)S(1)}, u32[]{:S(2)}, u32[]{:S(2)}) collective-permute-start(bf16[256,128]{1,0:T(8,128)(2,1)S(1)} %fusion), channel_id=1, source_target_pairs={{0,12},{2,14},{4,0},{6,2},{8,4},{10,6},{12,8},{14,10},{1,13},{3,15... | collective-permute-start | bytes 196616 | tf_op jit(solution)/shard_map/ppermute | solution.py:17
  39.1 1.1 %collective-permute-done.9 = bf16[256,128]{1,0:T(8,128)(2,1)S(1)} collective-permute-done((bf16[256,128]{1,0:T(8,128)(2,1)S(1)}, bf16[256,128]{1,0:T(8,128)(2,1)S(1)}, u32[]{:S(2)}, u32[]{:S(2)}) %collective-permute-start.9) | collective-permute-done | bytes 65568 | tf_op jit(solution)/shard_map/ppermute | solution.py:17
  41.6 1.2 %collective-permute-done.15 = bf16[256,128]{1,0:T(8,128)(2,1)S(1)} collective-permute-done((bf16[256,128]{1,0:T(8,128)(2,1)S(1)}, bf16[256,128]{1,0:T(8,128)(2,1)S(1)}, u32[]{:S(2)}, u32[]{:S(2)}) %collective-permute-start.15) | collective-permute-done | bytes 65568 | tf_op jit(solution)/shard_map/ppermute | solution.py:17
  42.8 0.7 %fusion.12 = (bf16[128,512]{1,0:T(8,128)(2,1)}, bf16[128,512]{1,0:T(8,128)(2,1)}) fusion(bf16[256,512]{1,0:T(8,128)(2,1)S(1)} %pad_maximum_fusion), kind=kLoop, calls=%fused_computation.29 | loop fusion | bytes 524288 | tf_op jit(solution)/shard_map/slice | solution.py:133
  (45 shorter events, 2.3 us)
Async XLA Ops:
  1.5 7.7 %collective-permute-start.6 = (bf16[256,128]{1,0:T(8,128)(2,1)S(1)}, bf16[256,128]{1,0:T(8,128)(2,1)S(1)}, u32[]{:S(2)}, u32[]{:S(2)}) collective-permute-start(bf16[256,128]{1,0:T(8,128)(2,1)S(1)} %pad_maximum_fusion.8), channel_id=1, source_target_pairs={{0,4},{2,6},{4,8},{6,10},{8,12},{10,14},{12,0},{14,2},{1,5},{3,7},... | collective-permute-start | bytes 196616 | tf_op jit(solution)/shard_map/ppermute | solution.py:17
  4.7 6.8 %collective-permute-start.4 = (bf16[256,128]{1,0:T(8,128)(2,1)S(1)}, bf16[256,128]{1,0:T(8,128)(2,1)S(1)}, u32[]{:S(2)}, u32[]{:S(2)}) collective-permute-start(bf16[256,128]{1,0:T(8,128)(2,1)S(1)} %pad_maximum_fusion.7), channel_id=1, source_target_pairs={{0,4},{2,6},{4,8},{6,10},{8,12},{10,14},{12,0},{14,2},{1,5},{3,7},... | collective-permute-start | bytes 196616 | tf_op jit(solution)/shard_map/ppermute | solution.py:17
  6.2 12.1 %copy-start.3 = (bf16[128,2048]{1,0:T(8,128)(2,1)S(1)}, bf16[128,2048]{1,0:T(8,128)(2,1)}, u32[]{:S(2)}) copy-start(bf16[128,2048]{1,0:T(8,128)(2,1)} %do_ref.7) | copy-start | bytes 1572868
  6.2 6.7 %collective-permute-start.2 = (bf16[256,128]{1,0:T(8,128)(2,1)S(1)}, bf16[256,128]{1,0:T(8,128)(2,1)S(1)}, u32[]{:S(2)}, u32[]{:S(2)}) collective-permute-start(bf16[256,128]{1,0:T(8,128)(2,1)S(1)} %pad_maximum_fusion.6), channel_id=1, source_target_pairs={{0,4},{2,6},{4,8},{6,10},{8,12},{10,14},{12,0},{14,2},{1,5},{3,7},... | collective-permute-start | bytes 196616 | tf_op jit(solution)/shard_map/ppermute | solution.py:17
  7.9 6.8 %collective-permute-start = (bf16[256,128]{1,0:T(8,128)(2,1)S(1)}, bf16[256,128]{1,0:T(8,128)(2,1)S(1)}, u32[]{:S(2)}, u32[]{:S(2)}) collective-permute-start(bf16[256,128]{1,0:T(8,128)(2,1)S(1)} %pad_maximum_fusion.5), channel_id=1, source_target_pairs={{0,4},{2,6},{4,8},{6,10},{8,12},{10,14},{12,0},{14,2},{1,5},{3,7},... | collective-permute-start | bytes 196616 | tf_op jit(solution)/shard_map/ppermute | solution.py:17
  8.0 10.4 %copy-start.2 = (bf16[128,2048]{1,0:T(8,128)(2,1)S(1)}, bf16[128,2048]{1,0:T(8,128)(2,1)}, u32[]{:S(2)}) copy-start(bf16[128,2048]{1,0:T(8,128)(2,1)} %q_ref.7) | copy-start | bytes 1572868
  9.3 9.1 %collective-permute-start.7 = (bf16[512,128]{1,0:T(8,128)(2,1)S(1)}, bf16[512,128]{1,0:T(8,128)(2,1)S(1)}, u32[]{:S(2)}, u32[]{:S(2)}) collective-permute-start(bf16[512,128]{1,0:T(8,128)(2,1)S(1)} %pad_maximum_fusion.4), channel_id=1, source_target_pairs={{0,2},{2,4},{4,6},{6,8},{8,10},{10,12},{12,14},{14,0},{1,3},{3,5},... | collective-permute-start | bytes 393224 | tf_op jit(solution)/shard_map/ppermute | solution.py:17
  11.4 10.7 %collective-permute-start.5 = (bf16[512,128]{1,0:T(8,128)(2,1)S(1)}, bf16[512,128]{1,0:T(8,128)(2,1)S(1)}, u32[]{:S(2)}, u32[]{:S(2)}) collective-permute-start(bf16[512,128]{1,0:T(8,128)(2,1)S(1)} %pad_maximum_fusion.3), channel_id=1, source_target_pairs={{0,2},{2,4},{4,6},{6,8},{8,10},{10,12},{12,14},{14,0},{1,3},{3,5},... | collective-permute-start | bytes 393224 | tf_op jit(solution)/shard_map/ppermute | solution.py:17
  13.0 5.4 %copy-start = (bf16[128,512]{1,0:T(8,128)(2,1)S(1)}, bf16[128,512]{1,0:T(8,128)(2,1)}, u32[]{:S(2)}) copy-start(bf16[128,512]{1,0:T(8,128)(2,1)} %k_ref.7) | copy-start | bytes 393220
  13.0 5.4 %copy-start.1 = (bf16[128,512]{1,0:T(8,128)(2,1)S(1)}, bf16[128,512]{1,0:T(8,128)(2,1)}, u32[]{:S(2)}) copy-start(bf16[128,512]{1,0:T(8,128)(2,1)} %v_ref.7) | copy-start | bytes 393220
  13.0 13.3 %collective-permute-start.3 = (bf16[512,128]{1,0:T(8,128)(2,1)S(1)}, bf16[512,128]{1,0:T(8,128)(2,1)S(1)}, u32[]{:S(2)}, u32[]{:S(2)}) collective-permute-start(bf16[512,128]{1,0:T(8,128)(2,1)S(1)} %pad_maximum_fusion.2), channel_id=1, source_target_pairs={{0,2},{2,4},{4,6},{6,8},{8,10},{10,12},{12,14},{14,0},{1,3},{3,5},... | collective-permute-start | bytes 393224 | tf_op jit(solution)/shard_map/ppermute | solution.py:17
  14.7 3.7 %copy-start.4 = (s32[4]{0:T(128)S(1)}, s32[4]{0:T(128)}, u32[]{:S(2)}) copy-start(s32[4]{0:T(128)} %lens_ref.7) | copy-start | bytes 52
  14.7 14.6 %collective-permute-start.1 = (bf16[512,128]{1,0:T(8,128)(2,1)S(1)}, bf16[512,128]{1,0:T(8,128)(2,1)S(1)}, u32[]{:S(2)}, u32[]{:S(2)}) collective-permute-start(bf16[512,128]{1,0:T(8,128)(2,1)S(1)} %pad_maximum_fusion.1), channel_id=1, source_target_pairs={{0,2},{2,4},{4,6},{6,8},{8,10},{10,12},{12,14},{14,0},{1,3},{3,5},... | collective-permute-start | bytes 393224 | tf_op jit(solution)/shard_map/ppermute | solution.py:17
  21.0 12.7 %collective-permute-start.8 = (bf16[512,128]{1,0:T(8,128)(2,1)S(1)}, bf16[512,128]{1,0:T(8,128)(2,1)S(1)}, u32[]{:S(2)}, u32[]{:S(2)}) collective-permute-start(bf16[512,128]{1,0:T(8,128)(2,1)S(1)} %get-tuple-element.33), channel_id=1, source_target_pairs={{0,14},{2,0},{4,2},{6,4},{8,6},{10,8},{12,10},{14,12},{1,15},{3,1}... | collective-permute-start | bytes 393224 | tf_op jit(solution)/shard_map/ppermute | solution.py:17
  24.8 9.8 %collective-permute-start.10 = (bf16[512,128]{1,0:T(8,128)(2,1)S(1)}, bf16[512,128]{1,0:T(8,128)(2,1)S(1)}, u32[]{:S(2)}, u32[]{:S(2)}) collective-permute-start(bf16[512,128]{1,0:T(8,128)(2,1)S(1)} %get-tuple-element.36), channel_id=1, source_target_pairs={{0,14},{2,0},{4,2},{6,4},{8,6},{10,8},{12,10},{14,12},{1,15},{3,1}... | collective-permute-start | bytes 393224 | tf_op jit(solution)/shard_map/ppermute | solution.py:17
  29.0 8.1 %collective-permute-start.12 = (bf16[512,128]{1,0:T(8,128)(2,1)S(1)}, bf16[512,128]{1,0:T(8,128)(2,1)S(1)}, u32[]{:S(2)}, u32[]{:S(2)}) collective-permute-start(bf16[512,128]{1,0:T(8,128)(2,1)S(1)} %get-tuple-element.39), channel_id=1, source_target_pairs={{0,14},{2,0},{4,2},{6,4},{8,6},{10,8},{12,10},{14,12},{1,15},{3,1}... | collective-permute-start | bytes 393224 | tf_op jit(solution)/shard_map/ppermute | solution.py:17
  31.9 6.4 %collective-permute-start.14 = (bf16[512,128]{1,0:T(8,128)(2,1)S(1)}, bf16[512,128]{1,0:T(8,128)(2,1)S(1)}, u32[]{:S(2)}, u32[]{:S(2)}) collective-permute-start(bf16[512,128]{1,0:T(8,128)(2,1)S(1)} %get-tuple-element.42), channel_id=1, source_target_pairs={{0,14},{2,0},{4,2},{6,4},{8,6},{10,8},{12,10},{14,12},{1,15},{3,1}... | collective-permute-start | bytes 393224 | tf_op jit(solution)/shard_map/ppermute | solution.py:17
  33.8 6.4 %collective-permute-start.9 = (bf16[256,128]{1,0:T(8,128)(2,1)S(1)}, bf16[256,128]{1,0:T(8,128)(2,1)S(1)}, u32[]{:S(2)}, u32[]{:S(2)}) collective-permute-start(bf16[256,128]{1,0:T(8,128)(2,1)S(1)} %fusion.9), channel_id=1, source_target_pairs={{0,12},{2,14},{4,0},{6,2},{8,4},{10,6},{12,8},{14,10},{1,13},{3,15... | collective-permute-start | bytes 196616 | tf_op jit(solution)/shard_map/ppermute | solution.py:17
  34.6 6.3 %collective-permute-start.11 = (bf16[256,128]{1,0:T(8,128)(2,1)S(1)}, bf16[256,128]{1,0:T(8,128)(2,1)S(1)}, u32[]{:S(2)}, u32[]{:S(2)}) collective-permute-start(bf16[256,128]{1,0:T(8,128)(2,1)S(1)} %fusion.6), channel_id=1, source_target_pairs={{0,12},{2,14},{4,0},{6,2},{8,4},{10,6},{12,8},{14,10},{1,13},{3,15... | collective-permute-start | bytes 196616 | tf_op jit(solution)/shard_map/ppermute | solution.py:17
  37.1 4.5 %collective-permute-start.13 = (bf16[256,128]{1,0:T(8,128)(2,1)S(1)}, bf16[256,128]{1,0:T(8,128)(2,1)S(1)}, u32[]{:S(2)}, u32[]{:S(2)}) collective-permute-start(bf16[256,128]{1,0:T(8,128)(2,1)S(1)} %fusion.3), channel_id=1, source_target_pairs={{0,12},{2,14},{4,0},{6,2},{8,4},{10,6},{12,8},{14,10},{1,13},{3,15... | collective-permute-start | bytes 196616 | tf_op jit(solution)/shard_map/ppermute | solution.py:17
  38.4 4.3 %collective-permute-start.15 = (bf16[256,128]{1,0:T(8,128)(2,1)S(1)}, bf16[256,128]{1,0:T(8,128)(2,1)S(1)}, u32[]{:S(2)}, u32[]{:S(2)}) collective-permute-start(bf16[256,128]{1,0:T(8,128)(2,1)S(1)} %fusion), channel_id=1, source_target_pairs={{0,12},{2,14},{4,0},{6,2},{8,4},{10,6},{12,8},{14,10},{1,13},{3,15... | collective-permute-start | bytes 196616 | tf_op jit(solution)/shard_map/ppermute | solution.py:17

commit v3 on v1

v3 whole, which is shorter than its diff:
```python
import functools
import math

import jax
import jax.numpy as jnp
from jax import lax
from jax.experimental import pallas as pl
from jax.experimental.pallas import tpu as pltpu
from jax.sharding import PartitionSpec as P

HEAD = 128
MASKED = -1e30
LOG2E = 1.4426950408889634


def shift(value, by):
    peers = lax.axis_size("cp")
    return lax.ppermute(value, "cp", [(i, (i + by) % peers) for i in range(peers)])


def dot(a, b, contract):
    return lax.dot_general(a, b, (contract, ((), ())), preferred_element_type=jnp.float32)


def stacked(block):
    heads = block.shape[1] // HEAD
    return jnp.concatenate([block[:, i * HEAD:(i + 1) * HEAD] for i in range(heads)], axis=0)


def attention_kernel(tok, heads_of, wide, lens_ref, pos_ref, q_ref, do_ref, k_ref, v_ref, *rest):
    count = len(heads_of)
    windows, outs = rest[:2 * count], rest[2 * count:]
    o_ref, dq_ref, own_ref, gmid_ref, gnear_ref = outs
    heads = wide // HEAD
    scale = 1.0 / math.sqrt(HEAD)
    start = pos_ref[0]
    query_pos = start + lax.broadcasted_iota(jnp.int32, (1, tok), 1)

    def place(d, carry):
        end, low = carry
        end = end + lens_ref[d]
        return end, jnp.where(end <= query_pos, end, low)

    _, low = lax.fori_loop(0, lens_ref.shape[0], place, (jnp.int32(0), jnp.zeros((1, tok), jnp.int32)))
    rel = lax.broadcasted_iota(jnp.int32, (4 * tok, tok), 0) - 3 * tok
    bias = jnp.where((rel >= low - start) & (rel <= query_pos - start), 0.0, MASKED)
    bias = jnp.concatenate([bias] * heads, axis=1)
    for c, (head, near_at, mid_at) in enumerate(heads_of):
        near_ref, mid_ref = windows[2 * c:2 * c + 2]
        near_kv = slice(near_at * HEAD, (near_at + 1) * HEAD)
        mid_kv = slice(mid_at * HEAD, (mid_at + 1) * HEAD)
        kv = slice(c * HEAD, (c + 1) * HEAD)
        mine = slice(head * HEAD, (head + 1) * HEAD)
        cols = slice(head * wide, (head + 1) * wide)
        keys = jnp.concatenate(
            [near_ref[2 * tok:3 * tok, near_kv], mid_ref[:tok, mid_kv], near_ref[:tok, near_kv], k_ref[:, mine]], axis=0
        )
        values = jnp.concatenate(
            [near_ref[3 * tok:, near_kv], mid_ref[tok:, mid_kv], near_ref[tok:2 * tok, near_kv], v_ref[:, mine]], axis=0
        )
        q = stacked(q_ref[:, cols])
        do = stacked(do_ref[:, cols])
        s = dot(keys, q, ((1,), (1,))) * (scale * LOG2E) + bias
        dp = dot(values, do, ((1,), (1,)))
        e = jnp.exp2(s - jnp.max(s, axis=0, keepdims=True))
        p = e * (1.0 / jnp.sum(e, axis=0, keepdims=True))
        p_low = p.astype(jnp.bfloat16)
        delta = jnp.sum(p * dp, axis=0, keepdims=True)
        ds = (p * (dp - delta)).astype(jnp.bfloat16)
        ot = dot(values, p_low, ((0,), (0,)))
        dqt = dot(keys, ds, ((0,), (0,))) * scale
        for i in range(heads):
            to = slice(c * wide + i * HEAD, c * wide + (i + 1) * HEAD)
            o_ref[:, to] = ot[:, i * tok:(i + 1) * tok].T.astype(o_ref.dtype)
            dq_ref[:, to] = dqt[:, i * tok:(i + 1) * tok].T.astype(dq_ref.dtype)
        dv = dot(p_low, do, ((1,), (0,)))
        dk = dot(ds, q, ((1,), (0,))) * scale
        gnear_ref[:tok, kv] = dk[2 * tok:3 * tok].astype(gnear_ref.dtype)
        gnear_ref[tok:2 * tok, kv] = dv[2 * tok:3 * tok].astype(gnear_ref.dtype)
        gnear_ref[2 * tok:3 * tok, kv] = dk[:tok].astype(gnear_ref.dtype)
        gnear_ref[3 * tok:, kv] = dv[:tok].astype(gnear_ref.dtype)
        gmid_ref[:tok, kv] = dk[tok:2 * tok]
        gmid_ref[tok:, kv] = dv[tok:2 * tok]
        own_ref[:tok, kv] = dk[3 * tok:]
        own_ref[tok:, kv] = dv[3 * tok:]


def attend(doc_lengths, start, queries, out_grad, keys, values, windows, heads_of):
    tok, width = queries.shape
    wide = width // (keys.shape[1] // HEAD)
    count = len(heads_of)
    smem = pl.BlockSpec(memory_space=pltpu.SMEM)
    vmem = pl.BlockSpec(memory_space=pltpu.VMEM)
    f32, low = jnp.float32, queries.dtype
    return pl.pallas_call(
        functools.partial(attention_kernel, tok, heads_of, wide),
        in_specs=[smem, smem] + [vmem] * (4 + len(windows)),
        out_specs=[vmem] * 5,
        out_shape=[
            jax.ShapeDtypeStruct((tok, wide * count), low),
            jax.ShapeDtypeStruct((tok, wide * count), low),
            jax.ShapeDtypeStruct((2 * tok, HEAD * count), f32),
            jax.ShapeDtypeStruct((2 * tok, HEAD * count), f32),
            jax.ShapeDtypeStruct((4 * tok, HEAD * count), low),
        ],
        compiler_params=pltpu.CompilerParams(vmem_limit_bytes=24 * 1024 * 1024),
        cost_estimate=pl.CostEstimate(
            flops=160 * tok * tok * wide * count, bytes_accessed=8 * tok * width, transcendentals=0
        ),
    )(doc_lengths, start, queries, out_grad, keys, values, *windows)


def cat(parts, axis):
    return parts[0] if len(parts) == 1 else jnp.concatenate(parts, axis=axis)


def part_of(array, at, count=1):
    return array[:, at * HEAD:(at + count) * HEAD]


def shards(doc_lengths, queries, key_states, value_head_states, out_grad):
    tok = queries.shape[0]
    start = (lax.axis_index("cp") * tok).astype(jnp.int32).reshape(1)
    low = key_states.dtype
    count = key_states.shape[1] // HEAD
    single = [(h,) for h in range(count)]
    paired = [tuple(range(count - 2))] + single[count - 2:] if count > 2 else single
    mid, near = {}, {}
    for j, group in enumerate(single):
        with jax.named_scope(f"s1_{j}"):
            own = [part_of(x, group[0], len(group)) for x in (key_states, value_head_states)]
            got = shift(jnp.concatenate(own, axis=0), 2)
        mid.update({h: (got, i) for i, h in enumerate(group)})
    for j, group in enumerate(single):
        with jax.named_scope(f"s2_{j}"):
            own = [part_of(x, group[0], len(group)) for x in (key_states, value_head_states)]
            got = shift(jnp.concatenate(own + [cat([part_of(*mid[h]) for h in group], 1)], axis=0), 1)
        near.update({h: (got, i) for i, h in enumerate(group)})
    outs, dqs, parts = [], [], {}
    for j, group in enumerate(single):
        windows = [x for h in group for x in (near[h][0], mid[h][0])]
        heads_of = [(h, near[h][1], mid[h][1]) for h in group]
        with jax.named_scope(f"k_{j}"):
            o, dq, *grads = attend(
                doc_lengths, start, queries, out_grad, key_states, value_head_states, windows, heads_of
            )
        outs.append(o)
        dqs.append(dq)
        parts.update({h: [part_of(g, i) if len(group) > 1 else g for g in grads] for i, h in enumerate(group)})
    own, onward = {}, {}
    for j, group in enumerate(single):
        with jax.named_scope(f"b1_{j}"):
            back = shift(cat([parts[h][2] for h in group], 1), -1)
        for i, h in enumerate(group):
            got = part_of(back, i).astype(jnp.float32)
            own[h] = parts[h][0] + got[:2 * tok]
            onward[h] = (parts[h][1] + got[2 * tok:]).astype(low)
    total = []
    for j, group in enumerate(paired):
        with jax.named_scope(f"b2_{j}"):
            far = shift(cat([onward[h] for h in group], 1), -2)
        total.append((cat([own[h] for h in group], 1) + far.astype(jnp.float32)).astype(low))
    total = cat(total, 1)
    with jax.named_scope("out_o"):
        attended = cat(outs, 1)
    with jax.named_scope("out_q"):
        grad_queries = cat(dqs, 1)
    return attended, grad_queries, total[:tok], total[tok:]


def solution(mesh):
    part = P(("group", "cp"), "hd")
    return jax.shard_map(
        shards,
        mesh=mesh,
        in_specs=(P("group"), part, part, part, part),
        out_specs=(part, part, part, part),
        check_vma=False,
    )
```

time: 61.3 us -> 42.3 us (0.69)
  waiting for transfers between devices: 37.9 us -> 8.04 us
  starting transfers between devices: 11.2 us -> 22.1 us
  other arithmetic: 1.42 us -> 2.07 us
    ppermute x4 -> x15, waiting for transfers between devices: 37.9 us -> 8.04 us  [shift(): lax.ppermute(value, 'cp', [(i, (i + by) % peers) for i in range(peers)])]
    ppermute x4 -> x15, starting transfers between devices: 11.2 us -> 22.1 us  [shift(): lax.ppermute(value, 'cp', [(i, (i + by) % peers) for i in range(peers)])]
    unnamed x12 -> x10, local copies, waits for them, and re-layouts: 1.47 us -> 0.03 us
    slice x0 -> x1, local copies, waits for them, and re-layouts: none -> 0.9 us  [part_of(): return array[:, at * HEAD:(at + count) * HEAD]]
    concatenate x2 -> x12, other arithmetic: 1.06 us -> 1.8 us  [the longest x4 1.74 us: cat(): return parts[0] if len(parts) == 1 else jnp.concatenate(parts, axis=axis)]
    pallas_call x1 -> x4, Pallas kernels: 7.61 us -> 7.36 us  [attend(): pl.pallas_call(functools.partial(attention_kernel, tok, heads_of, wide),...]
  transfers between devices with their start and end apart: 4 -> 15, of which waited for: 4 -> 7; matrix products, arithmetic and copies ran while one was open for 0% -> 5% of each run, Pallas kernels for 0% -> 17%
where the time goes in v3:
time: 42.3 us; the launch traced here: 42.1 us
  starting transfers between devices  22.1 us (52%)
  waiting for transfers between devices  8.04 us (19%)
  Pallas kernels  7.36 us (17%)
  other arithmetic  2.07 us (5%)
  local copies, waits for them, and re-layouts  1.64 us (4%)
  between operations  0.83 us (2%)
    ppermute x15, starting transfers between devices, shift(): lax.ppermute(value, 'cp', [(i, (i + by) % peers) for i in range(peers)])  22.1 us
    ppermute x15, waiting for transfers between devices, shift(): lax.ppermute(value, 'cp', [(i, (i + by) % peers) for i in range(peers)])  8.04 us
    pallas_call x4, Pallas kernels, attend(): pl.pallas_call(functools.partial(attention_kernel, tok, heads_of, wide),...  7.36 us
    concatenate x4, other arithmetic, cat(): return parts[0] if len(parts) == 1 else jnp.concatenate(parts, axis=axis)  1.74 us
    slice x1, local copies, waits for them, and re-layouts, part_of(): return array[:, at * HEAD:(at + count) * HEAD]  0.9 us
  transfers between devices with their start and end apart: 15, of which 7 were waited for; matrix products, arithmetic and copies ran while one was open for 5% of the time, Pallas kernels for 17%

profile of v3, /device:TPU:0, one launch (start us, length us, event | category | flops | bytes accessed | tf_op | source)
XLA Modules:
  0.0 42.1 jit_solution(5005745663832843210)
XLA Ops:
  0.6 0.9 %fusion.10 = (bf16[128,128]{1,0:T(8,128)(2,1)S(1)}, bf16[128,128]{1,0:T(8,128)(2,1)S(1)}, bf16[128,128]{1,0:T(8,128)(2,1)S(1)}, bf16[128,128]{1,0:T(8,128)(2,1)S...) fusion(bf16[128,512]{1,0:T(8,128)(2,1)} %k_ref.7, ...), kind=kLoop, calls=%fused_computation.31 | loop fusion | bytes 524288 | tf_op jit(solution)/shard_map/s2_0/slice | solution.py:118
  1.5 3.1 %collective-permute-start = (bf16[256,128]{1,0:T(8,128)(2,1)S(1)}, bf16[256,128]{1,0:T(8,128)(2,1)S(1)}, u32[]{:S(2)}, u32[]{:S(2)}) collective-permute-start(bf16[256,128]{1,0:T(8,128)(2,1)S(1)} %pad_maximum_fusion.8), channel_id=1, source_target_pairs={{0,4},{2,6},{4,8},{6,10},{8,12},{10,14},{12,0},{14,2},{1,5},{3,7},... | collective-permute-start | bytes 196616 | tf_op jit(solution)/shard_map/s1_0/ppermute | solution.py:18
  4.7 1.6 %collective-permute-start.2 = (bf16[256,128]{1,0:T(8,128)(2,1)S(1)}, bf16[256,128]{1,0:T(8,128)(2,1)S(1)}, u32[]{:S(2)}, u32[]{:S(2)}) collective-permute-start(bf16[256,128]{1,0:T(8,128)(2,1)S(1)} %pad_maximum_fusion.9), channel_id=1, source_target_pairs={{0,4},{2,6},{4,8},{6,10},{8,12},{10,14},{12,0},{14,2},{1,5},{3,7},... | collective-permute-start | bytes 196616 | tf_op jit(solution)/shard_map/s1_1/ppermute | solution.py:18
  6.2 1.6 %collective-permute-start.4 = (bf16[256,128]{1,0:T(8,128)(2,1)S(1)}, bf16[256,128]{1,0:T(8,128)(2,1)S(1)}, u32[]{:S(2)}, u32[]{:S(2)}) collective-permute-start(bf16[256,128]{1,0:T(8,128)(2,1)S(1)} %pad_maximum_fusion.10), channel_id=1, source_target_pairs={{0,4},{2,6},{4,8},{6,10},{8,12},{10,14},{12,0},{14,2},{1,5},{3,7},... | collective-permute-start | bytes 196616 | tf_op jit(solution)/shard_map/s1_2/ppermute | solution.py:18
  8.0 1.3 %collective-permute-done.rest_1_ = bf16[256,128]{1,0:T(8,128)(2,1)S(1)} collective-permute-done((bf16[256,128]{1,0:T(8,128)(2,1)S(1)}, bf16[256,128]{1,0:T(8,128)(2,1)S(1)}, u32[]{:S(2)}, u32[]{:S(2)}) %collective-permute-start) | collective-permute-done | bytes 65568 | tf_op jit(solution)/shard_map/s1_0/ppermute | solution.py:18
  9.3 2.0 %collective-permute-start.1 = (bf16[512,128]{1,0:T(8,128)(2,1)S(1)}, bf16[512,128]{1,0:T(8,128)(2,1)S(1)}, u32[]{:S(2)}, u32[]{:S(2)}) collective-permute-start(bf16[512,128]{1,0:T(8,128)(2,1)S(1)} %pad_maximum_fusion.3), channel_id=1, source_target_pairs={{0,2},{2,4},{4,6},{6,8},{8,10},{10,12},{12,14},{14,0},{1,3},{3,5},... | collective-permute-start | bytes 393224 | tf_op jit(solution)/shard_map/s2_0/ppermute | solution.py:18
  11.4 1.5 %collective-permute-start.3 = (bf16[512,128]{1,0:T(8,128)(2,1)S(1)}, bf16[512,128]{1,0:T(8,128)(2,1)S(1)}, u32[]{:S(2)}, u32[]{:S(2)}) collective-permute-start(bf16[512,128]{1,0:T(8,128)(2,1)S(1)} %pad_maximum_fusion.4), channel_id=1, source_target_pairs={{0,2},{2,4},{4,6},{6,8},{8,10},{10,12},{12,14},{14,0},{1,3},{3,5},... | collective-permute-start | bytes 393224 | tf_op jit(solution)/shard_map/s2_1/ppermute | solution.py:18
  13.0 1.6 %collective-permute-start.5 = (bf16[512,128]{1,0:T(8,128)(2,1)S(1)}, bf16[512,128]{1,0:T(8,128)(2,1)S(1)}, u32[]{:S(2)}, u32[]{:S(2)}) collective-permute-start(bf16[512,128]{1,0:T(8,128)(2,1)S(1)} %pad_maximum_fusion.5), channel_id=1, source_target_pairs={{0,2},{2,4},{4,6},{6,8},{8,10},{10,12},{12,14},{14,0},{1,3},{3,5},... | collective-permute-start | bytes 393224 | tf_op jit(solution)/shard_map/s2_2/ppermute | solution.py:18
  14.7 1.5 %collective-permute-start.7 = (bf16[512,128]{1,0:T(8,128)(2,1)S(1)}, bf16[512,128]{1,0:T(8,128)(2,1)S(1)}, u32[]{:S(2)}, u32[]{:S(2)}) collective-permute-start(bf16[512,128]{1,0:T(8,128)(2,1)S(1)} %pad_maximum_fusion.6), channel_id=1, source_target_pairs={{0,2},{2,4},{4,6},{6,8},{8,10},{10,12},{12,14},{14,0},{1,3},{3,5},... | collective-permute-start | bytes 393224 | tf_op jit(solution)/shard_map/s2_3/ppermute | solution.py:18
  16.2 2.2 %collective-permute-done.1.rest_0_ = bf16[512,128]{1,0:T(8,128)(2,1)S(1)} collective-permute-done((bf16[512,128]{1,0:T(8,128)(2,1)S(1)}, bf16[512,128]{1,0:T(8,128)(2,1)S(1)}, u32[]{:S(2)}, u32[]{:S(2)}) %collective-permute-start.1) | collective-permute-done | bytes 131104 | tf_op jit(solution)/shard_map/s2_0/ppermute | solution.py:18
  18.4 1.8 %k_0.1 = (bf16[128,512]{1,0:T(8,128)(2,1)S(1)}, bf16[128,512]{1,0:T(8,128)(2,1)S(1)}, f32[256,128]{1,0:T(8,128)S(1)}, f32[256,128]{1,0:T(8,128)S(1)}, bf16[512,128]{1,0:T(8,128)(2,1)S(1)}) custom-call(s32[4]{0:T(128)S(1)} %copy-done.4, s32[1]{0:T(128)} %bitcast.pos_ref, bf16[128,2048]{1,0:T(8,128)(2,1)S(1)} %copy-done.2, bf16[128,2048]{1,0:T(8,128)(2,1)S(1)} %copy-done.3, ...), custom_call_target="tpu_custom_call" | custom-call | flops 1342177280 | bytes 2097152 | tf_op jit(solution)/shard_map/k_0/pallas_call | solution.py:95
  20.3 1.1 %collective-permute-start.8 = (bf16[512,128]{1,0:T(8,128)(2,1)S(1)}, bf16[512,128]{1,0:T(8,128)(2,1)S(1)}, u32[]{:S(2)}, u32[]{:S(2)}) collective-permute-start(bf16[512,128]{1,0:T(8,128)(2,1)S(1)} %get-tuple-element.33), channel_id=1, source_target_pairs={{0,14},{2,0},{4,2},{6,4},{8,6},{10,8},{12,10},{14,12},{1,15},{3,1}... | collective-permute-start | bytes 393224 | tf_op jit(solution)/shard_map/b1_0/ppermute | solution.py:18
  21.4 1.8 %k_1.1 = (bf16[128,512]{1,0:T(8,128)(2,1)S(1)}, bf16[128,512]{1,0:T(8,128)(2,1)S(1)}, f32[256,128]{1,0:T(8,128)S(1)}, f32[256,128]{1,0:T(8,128)S(1)}, bf16[512,128]{1,0:T(8,128)(2,1)S(1)}) custom-call(s32[4]{0:T(128)S(1)} %copy-done.4, s32[1]{0:T(128)} %bitcast.pos_ref, bf16[128,2048]{1,0:T(8,128)(2,1)S(1)} %copy-done.2, bf16[128,2048]{1,0:T(8,128)(2,1)S(1)} %copy-done.3, ...), custom_call_target="tpu_custom_call" | custom-call | flops 1342177280 | bytes 2097152 | tf_op jit(solution)/shard_map/k_1/pallas_call | solution.py:95
  23.2 1.7 %collective-permute-start.9 = (bf16[512,128]{1,0:T(8,128)(2,1)S(1)}, bf16[512,128]{1,0:T(8,128)(2,1)S(1)}, u32[]{:S(2)}, u32[]{:S(2)}) collective-permute-start(bf16[512,128]{1,0:T(8,128)(2,1)S(1)} %get-tuple-element.35), channel_id=1, source_target_pairs={{0,14},{2,0},{4,2},{6,4},{8,6},{10,8},{12,10},{14,12},{1,15},{3,1}... | collective-permute-start | bytes 393224 | tf_op jit(solution)/shard_map/b1_1/ppermute | solution.py:18
  24.9 1.8 %k_2.1 = (bf16[128,512]{1,0:T(8,128)(2,1)S(1)}, bf16[128,512]{1,0:T(8,128)(2,1)S(1)}, f32[256,128]{1,0:T(8,128)S(1)}, f32[256,128]{1,0:T(8,128)S(1)}, bf16[512,128]{1,0:T(8,128)(2,1)S(1)}) custom-call(s32[4]{0:T(128)S(1)} %copy-done.4, s32[1]{0:T(128)} %bitcast.pos_ref, bf16[128,2048]{1,0:T(8,128)(2,1)S(1)} %copy-done.2, bf16[128,2048]{1,0:T(8,128)(2,1)S(1)} %copy-done.3, ...), custom_call_target="tpu_custom_call" | custom-call | flops 1342177280 | bytes 2097152 | tf_op jit(solution)/shard_map/k_2/pallas_call | solution.py:95
  26.7 1.0 %collective-permute-start.11 = (bf16[512,128]{1,0:T(8,128)(2,1)S(1)}, bf16[512,128]{1,0:T(8,128)(2,1)S(1)}, u32[]{:S(2)}, u32[]{:S(2)}) collective-permute-start(bf16[512,128]{1,0:T(8,128)(2,1)S(1)} %get-tuple-element.39), channel_id=1, source_target_pairs={{0,14},{2,0},{4,2},{6,4},{8,6},{10,8},{12,10},{14,12},{1,15},{3,1}... | collective-permute-start | bytes 393224 | tf_op jit(solution)/shard_map/b1_2/ppermute | solution.py:18
  27.7 1.8 %k_3.1 = (bf16[128,512]{1,0:T(8,128)(2,1)S(1)}, bf16[128,512]{1,0:T(8,128)(2,1)S(1)}, f32[256,128]{1,0:T(8,128)S(1)}, f32[256,128]{1,0:T(8,128)S(1)}, bf16[512,128]{1,0:T(8,128)(2,1)S(1)}) custom-call(s32[4]{0:T(128)S(1)} %copy-done.4, s32[1]{0:T(128)} %bitcast.pos_ref, bf16[128,2048]{1,0:T(8,128)(2,1)S(1)} %copy-done.2, bf16[128,2048]{1,0:T(8,128)(2,1)S(1)} %copy-done.3, ...), custom_call_target="tpu_custom_call" | custom-call | flops 1342177280 | bytes 2097152 | tf_op jit(solution)/shard_map/k_3/pallas_call | solution.py:95
  29.6 1.2 %collective-permute-start.13 = (bf16[512,128]{1,0:T(8,128)(2,1)S(1)}, bf16[512,128]{1,0:T(8,128)(2,1)S(1)}, u32[]{:S(2)}, u32[]{:S(2)}) collective-permute-start(bf16[512,128]{1,0:T(8,128)(2,1)S(1)} %get-tuple-element.42), channel_id=1, source_target_pairs={{0,14},{2,0},{4,2},{6,4},{8,6},{10,8},{12,10},{14,12},{1,15},{3,1}... | collective-permute-start | bytes 393224 | tf_op jit(solution)/shard_map/b1_3/ppermute | solution.py:18
  32.6 1.1 %collective-permute-start.10 = (bf16[256,256]{1,0:T(8,128)(2,1)S(1)}, bf16[256,256]{1,0:T(8,128)(2,1)S(1)}, u32[]{:S(2)}, u32[]{:S(2)}) collective-permute-start(bf16[256,256]{1,0:T(8,128)(2,1)S(1)} %pad_maximum_fusion.7), channel_id=1, source_target_pairs={{0,12},{2,14},{4,0},{6,2},{8,4},{10,6},{12,8},{14,10},{1,13},{3,15... | collective-permute-start | bytes 393224 | tf_op jit(solution)/shard_map/b2_0/ppermute | solution.py:18
  34.2 1.7 %collective-permute-start.12 = (bf16[256,128]{1,0:T(8,128)(2,1)S(1)}, bf16[256,128]{1,0:T(8,128)(2,1)S(1)}, u32[]{:S(2)}, u32[]{:S(2)}) collective-permute-start(bf16[256,128]{1,0:T(8,128)(2,1)S(1)} %fusion.4), channel_id=1, source_target_pairs={{0,12},{2,14},{4,0},{6,2},{8,4},{10,6},{12,8},{14,10},{1,13},{3,15... | collective-permute-start | bytes 196616 | tf_op jit(solution)/shard_map/b2_1/ppermute | solution.py:18
  35.9 1.0 %collective-permute-done.13 = bf16[512,128]{1,0:T(8,128)(2,1)S(1)} collective-permute-done((bf16[512,128]{1,0:T(8,128)(2,1)S(1)}, bf16[512,128]{1,0:T(8,128)(2,1)S(1)}, u32[]{:S(2)}, u32[]{:S(2)}) %collective-permute-start.13) | collective-permute-done | bytes 131104 | tf_op jit(solution)/shard_map/b1_3/ppermute | solution.py:18
  36.9 1.3 %collective-permute-start.14 = (bf16[256,128]{1,0:T(8,128)(2,1)S(1)}, bf16[256,128]{1,0:T(8,128)(2,1)S(1)}, u32[]{:S(2)}, u32[]{:S(2)}) collective-permute-start(bf16[256,128]{1,0:T(8,128)(2,1)S(1)} %fusion.1), channel_id=1, source_target_pairs={{0,12},{2,14},{4,0},{6,2},{8,4},{10,6},{12,8},{14,10},{1,13},{3,15... | collective-permute-start | bytes 196616 | tf_op jit(solution)/shard_map/b2_2/ppermute | solution.py:18
  38.2 1.1 %collective-permute-done.12 = bf16[256,128]{1,0:T(8,128)(2,1)S(1)} collective-permute-done((bf16[256,128]{1,0:T(8,128)(2,1)S(1)}, bf16[256,128]{1,0:T(8,128)(2,1)S(1)}, u32[]{:S(2)}, u32[]{:S(2)}) %collective-permute-start.12) | collective-permute-done | bytes 65568 | tf_op jit(solution)/shard_map/b2_1/ppermute | solution.py:18
  39.4 1.9 %collective-permute-done.14 = bf16[256,128]{1,0:T(8,128)(2,1)S(1)} collective-permute-done((bf16[256,128]{1,0:T(8,128)(2,1)S(1)}, bf16[256,128]{1,0:T(8,128)(2,1)S(1)}, u32[]{:S(2)}, u32[]{:S(2)}) %collective-permute-start.14) | collective-permute-done | bytes 65568 | tf_op jit(solution)/shard_map/b2_2/ppermute | solution.py:18
  (45 shorter events, 3.5 us)
Async XLA Ops:
  1.5 7.7 %collective-permute-start = (bf16[256,128]{1,0:T(8,128)(2,1)S(1)}, bf16[256,128]{1,0:T(8,128)(2,1)S(1)}, u32[]{:S(2)}, u32[]{:S(2)}) collective-permute-start(bf16[256,128]{1,0:T(8,128)(2,1)S(1)} %pad_maximum_fusion.8), channel_id=1, source_target_pairs={{0,4},{2,6},{4,8},{6,10},{8,12},{10,14},{12,0},{14,2},{1,5},{3,7},... | collective-permute-start | bytes 196616 | tf_op jit(solution)/shard_map/s1_0/ppermute | solution.py:18
  4.7 6.8 %collective-permute-start.2 = (bf16[256,128]{1,0:T(8,128)(2,1)S(1)}, bf16[256,128]{1,0:T(8,128)(2,1)S(1)}, u32[]{:S(2)}, u32[]{:S(2)}) collective-permute-start(bf16[256,128]{1,0:T(8,128)(2,1)S(1)} %pad_maximum_fusion.9), channel_id=1, source_target_pairs={{0,4},{2,6},{4,8},{6,10},{8,12},{10,14},{12,0},{14,2},{1,5},{3,7},... | collective-permute-start | bytes 196616 | tf_op jit(solution)/shard_map/s1_1/ppermute | solution.py:18
  6.2 12.1 %copy-start.3 = (bf16[128,2048]{1,0:T(8,128)(2,1)S(1)}, bf16[128,2048]{1,0:T(8,128)(2,1)}, u32[]{:S(2)}) copy-start(bf16[128,2048]{1,0:T(8,128)(2,1)} %do_ref.7) | copy-start | bytes 1572868
  6.2 6.7 %collective-permute-start.4 = (bf16[256,128]{1,0:T(8,128)(2,1)S(1)}, bf16[256,128]{1,0:T(8,128)(2,1)S(1)}, u32[]{:S(2)}, u32[]{:S(2)}) collective-permute-start(bf16[256,128]{1,0:T(8,128)(2,1)S(1)} %pad_maximum_fusion.10), channel_id=1, source_target_pairs={{0,4},{2,6},{4,8},{6,10},{8,12},{10,14},{12,0},{14,2},{1,5},{3,7},... | collective-permute-start | bytes 196616 | tf_op jit(solution)/shard_map/s1_2/ppermute | solution.py:18
  7.9 6.8 %collective-permute-start.6 = (bf16[256,128]{1,0:T(8,128)(2,1)S(1)}, bf16[256,128]{1,0:T(8,128)(2,1)S(1)}, u32[]{:S(2)}, u32[]{:S(2)}) collective-permute-start(bf16[256,128]{1,0:T(8,128)(2,1)S(1)} %pad_maximum_fusion.11), channel_id=1, source_target_pairs={{0,4},{2,6},{4,8},{6,10},{8,12},{10,14},{12,0},{14,2},{1,5},{3,7},... | collective-permute-start | bytes 196616 | tf_op jit(solution)/shard_map/s1_3/ppermute | solution.py:18
  8.0 10.4 %copy-start.2 = (bf16[128,2048]{1,0:T(8,128)(2,1)S(1)}, bf16[128,2048]{1,0:T(8,128)(2,1)}, u32[]{:S(2)}) copy-start(bf16[128,2048]{1,0:T(8,128)(2,1)} %q_ref.7) | copy-start | bytes 1572868
  9.3 9.1 %collective-permute-start.1 = (bf16[512,128]{1,0:T(8,128)(2,1)S(1)}, bf16[512,128]{1,0:T(8,128)(2,1)S(1)}, u32[]{:S(2)}, u32[]{:S(2)}) collective-permute-start(bf16[512,128]{1,0:T(8,128)(2,1)S(1)} %pad_maximum_fusion.3), channel_id=1, source_target_pairs={{0,2},{2,4},{4,6},{6,8},{8,10},{10,12},{12,14},{14,0},{1,3},{3,5},... | collective-permute-start | bytes 393224 | tf_op jit(solution)/shard_map/s2_0/ppermute | solution.py:18
  11.4 9.9 %collective-permute-start.3 = (bf16[512,128]{1,0:T(8,128)(2,1)S(1)}, bf16[512,128]{1,0:T(8,128)(2,1)S(1)}, u32[]{:S(2)}, u32[]{:S(2)}) collective-permute-start(bf16[512,128]{1,0:T(8,128)(2,1)S(1)} %pad_maximum_fusion.4), channel_id=1, source_target_pairs={{0,2},{2,4},{4,6},{6,8},{8,10},{10,12},{12,14},{14,0},{1,3},{3,5},... | collective-permute-start | bytes 393224 | tf_op jit(solution)/shard_map/s2_1/ppermute | solution.py:18
  13.0 5.4 %copy-start = (bf16[128,512]{1,0:T(8,128)(2,1)S(1)}, bf16[128,512]{1,0:T(8,128)(2,1)}, u32[]{:S(2)}) copy-start(bf16[128,512]{1,0:T(8,128)(2,1)} %k_ref.7) | copy-start | bytes 393220
  13.0 5.4 %copy-start.1 = (bf16[128,512]{1,0:T(8,128)(2,1)S(1)}, bf16[128,512]{1,0:T(8,128)(2,1)}, u32[]{:S(2)}) copy-start(bf16[128,512]{1,0:T(8,128)(2,1)} %v_ref.7) | copy-start | bytes 393220
  13.0 11.9 %collective-permute-start.5 = (bf16[512,128]{1,0:T(8,128)(2,1)S(1)}, bf16[512,128]{1,0:T(8,128)(2,1)S(1)}, u32[]{:S(2)}, u32[]{:S(2)}) collective-permute-start(bf16[512,128]{1,0:T(8,128)(2,1)S(1)} %pad_maximum_fusion.5), channel_id=1, source_target_pairs={{0,2},{2,4},{4,6},{6,8},{8,10},{10,12},{12,14},{14,0},{1,3},{3,5},... | collective-permute-start | bytes 393224 | tf_op jit(solution)/shard_map/s2_2/ppermute | solution.py:18
  14.7 3.7 %copy-start.4 = (s32[4]{0:T(128)S(1)}, s32[4]{0:T(128)}, u32[]{:S(2)}) copy-start(s32[4]{0:T(128)} %lens_ref.7) | copy-start | bytes 52
  14.7 13.0 %collective-permute-start.7 = (bf16[512,128]{1,0:T(8,128)(2,1)S(1)}, bf16[512,128]{1,0:T(8,128)(2,1)S(1)}, u32[]{:S(2)}, u32[]{:S(2)}) collective-permute-start(bf16[512,128]{1,0:T(8,128)(2,1)S(1)} %pad_maximum_fusion.6), channel_id=1, source_target_pairs={{0,2},{2,4},{4,6},{6,8},{8,10},{10,12},{12,14},{14,0},{1,3},{3,5},... | collective-permute-start | bytes 393224 | tf_op jit(solution)/shard_map/s2_3/ppermute | solution.py:18
  20.3 12.2 %collective-permute-start.8 = (bf16[512,128]{1,0:T(8,128)(2,1)S(1)}, bf16[512,128]{1,0:T(8,128)(2,1)S(1)}, u32[]{:S(2)}, u32[]{:S(2)}) collective-permute-start(bf16[512,128]{1,0:T(8,128)(2,1)S(1)} %get-tuple-element.33), channel_id=1, source_target_pairs={{0,14},{2,0},{4,2},{6,4},{8,6},{10,8},{12,10},{14,12},{1,15},{3,1}... | collective-permute-start | bytes 393224 | tf_op jit(solution)/shard_map/b1_0/ppermute | solution.py:18
  23.2 9.3 %collective-permute-start.9 = (bf16[512,128]{1,0:T(8,128)(2,1)S(1)}, bf16[512,128]{1,0:T(8,128)(2,1)S(1)}, u32[]{:S(2)}, u32[]{:S(2)}) collective-permute-start(bf16[512,128]{1,0:T(8,128)(2,1)S(1)} %get-tuple-element.35), channel_id=1, source_target_pairs={{0,14},{2,0},{4,2},{6,4},{8,6},{10,8},{12,10},{14,12},{1,15},{3,1}... | collective-permute-start | bytes 393224 | tf_op jit(solution)/shard_map/b1_1/ppermute | solution.py:18
  26.7 7.4 %collective-permute-start.11 = (bf16[512,128]{1,0:T(8,128)(2,1)S(1)}, bf16[512,128]{1,0:T(8,128)(2,1)S(1)}, u32[]{:S(2)}, u32[]{:S(2)}) collective-permute-start(bf16[512,128]{1,0:T(8,128)(2,1)S(1)} %get-tuple-element.39), channel_id=1, source_target_pairs={{0,14},{2,0},{4,2},{6,4},{8,6},{10,8},{12,10},{14,12},{1,15},{3,1}... | collective-permute-start | bytes 393224 | tf_op jit(solution)/shard_map/b1_2/ppermute | solution.py:18
  29.6 7.3 %collective-permute-start.13 = (bf16[512,128]{1,0:T(8,128)(2,1)S(1)}, bf16[512,128]{1,0:T(8,128)(2,1)S(1)}, u32[]{:S(2)}, u32[]{:S(2)}) collective-permute-start(bf16[512,128]{1,0:T(8,128)(2,1)S(1)} %get-tuple-element.42), channel_id=1, source_target_pairs={{0,14},{2,0},{4,2},{6,4},{8,6},{10,8},{12,10},{14,12},{1,15},{3,1}... | collective-permute-start | bytes 393224 | tf_op jit(solution)/shard_map/b1_3/ppermute | solution.py:18
  32.6 8.6 %collective-permute-start.10 = (bf16[256,256]{1,0:T(8,128)(2,1)S(1)}, bf16[256,256]{1,0:T(8,128)(2,1)S(1)}, u32[]{:S(2)}, u32[]{:S(2)}) collective-permute-start(bf16[256,256]{1,0:T(8,128)(2,1)S(1)} %pad_maximum_fusion.7), channel_id=1, source_target_pairs={{0,12},{2,14},{4,0},{6,2},{8,4},{10,6},{12,8},{14,10},{1,13},{3,15... | collective-permute-start | bytes 393224 | tf_op jit(solution)/shard_map/b2_0/ppermute | solution.py:18
  34.2 5.1 %collective-permute-start.12 = (bf16[256,128]{1,0:T(8,128)(2,1)S(1)}, bf16[256,128]{1,0:T(8,128)(2,1)S(1)}, u32[]{:S(2)}, u32[]{:S(2)}) collective-permute-start(bf16[256,128]{1,0:T(8,128)(2,1)S(1)} %fusion.4), channel_id=1, source_target_pairs={{0,12},{2,14},{4,0},{6,2},{8,4},{10,6},{12,8},{14,10},{1,13},{3,15... | collective-permute-start | bytes 196616 | tf_op jit(solution)/shard_map/b2_1/ppermute | solution.py:18
  36.9 4.3 %collective-permute-start.14 = (bf16[256,128]{1,0:T(8,128)(2,1)S(1)}, bf16[256,128]{1,0:T(8,128)(2,1)S(1)}, u32[]{:S(2)}, u32[]{:S(2)}) collective-permute-start(bf16[256,128]{1,0:T(8,128)(2,1)S(1)} %fusion.1), channel_id=1, source_target_pairs={{0,12},{2,14},{4,0},{6,2},{8,4},{10,6},{12,8},{14,10},{1,13},{3,15... | collective-permute-start | bytes 196616 | tf_op jit(solution)/shard_map/b2_2/ppermute | solution.py:18
